TPU v7x, 8 devices: a whole 2x2x1 slice. The times are simulated.
8 devices in a mesh: data: 2 (over z, y), pair: 4 (over x, core).
Axes of the slice: x: 2, y: 2, z: 1, core: 2. Of those that a mesh axis runs over, the one named last changes fastest.
Arguments:
- x_enc: bfloat16 [256, 256, 1024], P(('data', 'pair')), parts along dimension 0
- enc_len: int32 [256], P(('data', 'pair')), parts along dimension 0
- y_dec: bfloat16 [256, 96, 1024], P(('data', 'pair')), parts along dimension 0
- enc_wq: bfloat16 [2, 1024, 1024], replicated
- enc_wk: bfloat16 [2, 1024, 1024], replicated
- enc_wv: bfloat16 [2, 1024, 1024], replicated
- enc_wo: bfloat16 [2, 16, 64, 1024], replicated
- enc_w1: bfloat16 [2, 1024, 2816], replicated
- enc_w2: bfloat16 [2, 2816, 1024], replicated
- dec_wq: bfloat16 [2, 1024, 1024], replicated
- dec_wk: bfloat16 [2, 1024, 1024], replicated
- dec_wv: bfloat16 [2, 1024, 1024], replicated
- dec_wo: bfloat16 [2, 16, 64, 1024], replicated
- crs_wq: bfloat16 [2, 1024, 1024], replicated
- crs_wk: bfloat16 [2, 1024, 1024], replicated
- crs_wv: bfloat16 [2, 1024, 1024], replicated
- crs_wo: bfloat16 [2, 16, 64, 1024], replicated
- dec_w1: bfloat16 [2, 1024, 2816], replicated
- dec_w2: bfloat16 [2, 2816, 1024], replicated
Outputs:
- output: bfloat16 [256, 96, 1024], P(('data', 'pair')), parts along dimension 0
There are 2 independent parts. A program takes and returns all parts, laid end to end along the dimension named above; an argument that names none is the same for every part.
All inputs are finite; a program needn't handle non-finite values.
Results may differ from a plain program's by a relative error of at most 0.0122378.
Values are sent between devices in bfloat16 or wider.
A program may use at most 1 GiB of HBM per device.

v0:
```python
import jax
import jax.numpy as jnp
from jax import lax
from jax.sharding import PartitionSpec as P


def rms_norm(hidden):
    x_wide = hidden.astype(jnp.float32)
    inv_rms = lax.rsqrt(jnp.mean(x_wide * x_wide, axis=-1, keepdims=True) + 1e-6)
    return (x_wide * inv_rms).astype(jnp.bfloat16)


def project(source, weight):
    return jnp.dot(source, weight, preferred_element_type=jnp.float32).astype(jnp.bfloat16)


def add_to(hidden, update):
    return (hidden.astype(jnp.float32) + update).astype(jnp.bfloat16)


def key_mask(lengths, k_len):
    return (jnp.arange(k_len)[None, :] < lengths[:, None])[:, None, None, None, :]


def attend(query_rows, key_rows, value_rows, allowed, out_weight):
    num_heads, head_dim, d_model = out_weight.shape
    batch_rows, q_len = query_rows.shape[0], query_rows.shape[1]
    k_len = key_rows.shape[1]
    kv_heads = key_rows.shape[2] // head_dim
    q_per_kv = num_heads // kv_heads
    q_heads = query_rows.reshape(batch_rows, q_len, kv_heads, q_per_kv, head_dim)
    k_heads = key_rows.reshape(batch_rows, k_len, kv_heads, head_dim)
    v_heads = value_rows.reshape(batch_rows, k_len, kv_heads, head_dim)
    scores = jnp.einsum("bskrh,btkh->bkrst", q_heads, k_heads, preferred_element_type=jnp.float32) * head_dim ** -0.5
    scores = jnp.where(allowed, scores, -1e30)
    attn_probs = jax.nn.softmax(scores, axis=-1).astype(jnp.bfloat16)
    context = jnp.einsum("bkrst,btkh->bkrsh", attn_probs, v_heads, preferred_element_type=jnp.float32).astype(jnp.bfloat16)
    w_out = out_weight.reshape(kv_heads, q_per_kv, head_dim, d_model)
    return jnp.einsum("bkrsh,krhd->bsd", context, w_out, preferred_element_type=jnp.float32)


def feed_forward(hidden, w_up, w_down):
    normed = rms_norm(hidden)
    inner_act = jax.nn.gelu(jnp.dot(normed, w_up, preferred_element_type=jnp.float32)).astype(jnp.bfloat16)
    return add_to(hidden, jnp.dot(inner_act, w_down, preferred_element_type=jnp.float32))


def encode(x_enc, enc_len, enc_weights):
    enc_wq, enc_wk, enc_wv, enc_wo, enc_w1, enc_w2 = enc_weights
    allowed = key_mask(enc_len, x_enc.shape[1])
    hidden = x_enc
    for layer_idx in range(enc_wq.shape[0]):
        normed = rms_norm(hidden)
        attn_out = attend(project(normed, enc_wq[layer_idx]), project(normed, enc_wk[layer_idx]), project(normed, enc_wv[layer_idx]), allowed, enc_wo[layer_idx])
        hidden = feed_forward(add_to(hidden, attn_out), enc_w1[layer_idx], enc_w2[layer_idx])
    return rms_norm(hidden)


def decode(y_dec, cross_keys, cross_vals, partner_len, dec_weights):
    dec_wq, dec_wk, dec_wv, dec_wo, crs_wq, crs_wo, dec_w1, dec_w2 = dec_weights
    dec_len = y_dec.shape[1]
    causal = jnp.arange(dec_len)[:, None] >= jnp.arange(dec_len)[None, :]
    cross_ok = key_mask(partner_len, cross_keys[0].shape[1])
    hidden = y_dec
    for layer_idx in range(dec_wq.shape[0]):
        normed = rms_norm(hidden)
        self_out = attend(project(normed, dec_wq[layer_idx]), project(normed, dec_wk[layer_idx]), project(normed, dec_wv[layer_idx]), causal, dec_wo[layer_idx])
        hidden = add_to(hidden, self_out)
        cross_out = attend(project(rms_norm(hidden), crs_wq[layer_idx]), cross_keys[layer_idx], cross_vals[layer_idx], cross_ok, crs_wo[layer_idx])
        hidden = feed_forward(add_to(hidden, cross_out), dec_w1[layer_idx], dec_w2[layer_idx])
    return hidden


def solution(mesh):
    pair_size = mesh.shape["pair"]
    to_partner = [(source, (source + pair_size // 2) % pair_size) for source in range(pair_size)]
    row_spec = P(("data", "pair"))
    full_spec = P()

    def per_device(x_enc, enc_len, y_dec, enc_wq, enc_wk, enc_wv, enc_wo, enc_w1, enc_w2, dec_wq, dec_wk, dec_wv, dec_wo, crs_wq, crs_wk, crs_wv, crs_wo, dec_w1, dec_w2):
        enc_out = encode(x_enc, enc_len, (enc_wq, enc_wk, enc_wv, enc_wo, enc_w1, enc_w2))
        own_keys = [project(enc_out, crs_wk[layer_idx]) for layer_idx in range(crs_wk.shape[0])]
        own_vals = [project(enc_out, crs_wv[layer_idx]) for layer_idx in range(crs_wv.shape[0])]
        cross_keys, cross_vals, partner_len = lax.ppermute((own_keys, own_vals, enc_len), "pair", to_partner)
        return decode(y_dec, cross_keys, cross_vals, partner_len, (dec_wq, dec_wk, dec_wv, dec_wo, crs_wq, crs_wo, dec_w1, dec_w2))

    return jax.shard_map(per_device, mesh=mesh, in_specs=(row_spec, row_spec, row_spec) + (full_spec,) * 16, out_specs=row_spec, check_vma=False)
```

profile of v0, /device:TPU:0, one launch (start us, length us, event | category | flops | bytes accessed | tf_op | source)
XLA Modules:
  0.0 2461.3 jit_solution(1793617087162546369)
XLA Ops:
  11.9 24.1 fusion.158
  36.0 22.5 copy.35
  58.5 24.8 %fusion.161 = bf16[32,256,1024]{2,1,0:T(8,128)(2,1)} fusion(bf16[32,256,1024]{2,1,0:T(8,128)(2,1)} %param.19, f32[32,256]{1,0:T(8,128)S(1)} %add_rsqrt_fusion.4, bf16[2,1024,1024]{2,1,0:T(8,128)(2,1)} %param.22), kind=kOutput, calls=%fused_computation.177 | convolution fusion | flops 17213423616 | bytes 35684352 | tf_op jit(solution)/shard_map/dot_general | solution.py:14
  83.2 22.5 copy.36
  105.7 24.8 %fusion.164 = bf16[32,256,1024]{2,1,0:T(8,128)(2,1)} fusion(bf16[32,256,1024]{2,1,0:T(8,128)(2,1)} %param.19, f32[32,256]{1,0:T(8,128)S(1)} %add_rsqrt_fusion.4, bf16[2,1024,1024]{2,1,0:T(8,128)(2,1)} %param.24), kind=kOutput, calls=%fused_computation.178 | convolution fusion | flops 17213423616 | bytes 35684352 | tf_op jit(solution)/shard_map/dot_general | solution.py:14
  130.5 22.5 copy.37
  153.0 59.5 %bitcast_reduce_fusion.1 = (f32[32,16,256]{2,1,0:T(8,128)S(1)}, f32[32,16,256,256]{3,2,1,0:T(8,128)}) fusion(pred[32,256]{1,0:T(8,128)(4,1)S(1)} %copy-done.2, bf16[32,256,16,64]{1,3,2,0:T(8,128)(2,1)} %bitcast.576, bf16[32,256,16,64]{1,3,2,0:T(8,128)(2,1)} %bitcast.577), kind=kOutput, calls=%fused_computation.7 | convolution fusion | flops 4395499520 | bytes 168304640 | tf_op jit(solution)/shard_map/bskrh,btkh->bkrst/dot_general | solution.py:34
  212.5 41.2 %fusion.2 = f32[32,16,256]{2,1,0:T(8,128)S(1)} fusion(f32[32,16,256,256]{3,2,1,0:T(8,128)} %get-tuple-element.8, f32[32,16,256]{2,1,0:T(8,128)S(1)} %get-tuple-element.7, pred[32,256]{1,0:T(8,128)(4,1)S(1)} %copy-done.2), kind=kLoop, calls=%fused_computation.12 | loop fusion | flops 134086656 | bytes 135274496 | tf_op jit(solution)/shard_map/reduce_sum | solution.py:36
  253.7 68.3 %fusion.51 = (f32[32,256]{1,0:T(8,128)S(1)}, bf16[32,256,1024]{2,1,0:T(8,128)(2,1)}) fusion(bf16[2,16,64,1024]{3,2,1,0:T(8,128)(2,1)} %param.25, bf16[32,256,16,64]{1,3,2,0:T(8,128)(2,1)} %bitcast.587, f32[32,16,256]{2,1,0:T(8,128)S(1)} %fusion.2, f32[32,16,256]{2,1,0:T(8,128)S(1)} %get-tuple-element.7, f32[32,16,256,256]{3,2,1,0:T(8,128)} %get-tuple-element.8, ...), kind=kOutput, calls=%fused_computation.85 | convolution fusion | flops 21701320704 | bytes 187736064 | tf_op jit(solution)/shard_map/bkrsh,krhd->bsd/dot_general | solution.py:39
  322.0 73.5 %fusion.11.clone.1.clone.5 = bf16[32,256,2816]{2,1,0:T(8,128)(2,1)} fusion(bf16[32,256,1024]{2,1,0:T(8,128)(2,1)} %get-tuple-element.10, f32[32,256]{1,0:T(8,128)S(1)} %add_rsqrt_fusion.3, bf16[2,1024,2816]{2,1,0:T(8,128)(2,1)} %param.26), kind=kOutput, calls=%fused_computation.21.clone.clone.clone.clone.clone.2 | convolution fusion | flops 47477424128 | bytes 68714496 | tf_op jit(solution)/shard_map/dot_general | solution.py:44
  395.5 56.9 %fusion.54 = (f32[32,256]{1,0:T(8,128)S(1)}, bf16[32,256,1024]{2,1,0:T(8,128)(2,1)}) fusion(bf16[2,2816,1024]{2,1,0:T(8,128)(2,1)} %param.27, bf16[32,256,1024]{2,1,0:T(8,128)(2,1)} %get-tuple-element.10, bf16[32,256,2816]{2,1,0:T(8,128)(2,1)} %fusion.11.clone.1.clone.5), kind=kOutput, calls=%fused_computation.88 | convolution fusion | flops 47294963712 | bytes 85491712 | tf_op jit(solution)/shard_map/dot_general | solution.py:45
  452.5 24.2 fusion.170
  476.7 24.4 fusion.167
  501.1 24.1 fusion.173
  525.2 22.4 copy.39
  547.7 22.8 copy.38
  570.5 22.5 copy.40
  593.0 59.5 %bitcast_reduce_fusion = (f32[32,16,256]{2,1,0:T(8,128)S(1)}, f32[32,16,256,256]{3,2,1,0:T(8,128)}) fusion(pred[32,256]{1,0:T(8,128)(4,1)S(1)} %copy-done.3, bf16[32,256,16,64]{1,3,2,0:T(8,128)(2,1)} %bitcast.579, bf16[32,256,16,64]{1,3,2,0:T(8,128)(2,1)} %bitcast.578), kind=kOutput, calls=%fused_computation.3 | convolution fusion | flops 4395499520 | bytes 168304640 | tf_op jit(solution)/shard_map/bskrh,btkh->bkrst/dot_general | solution.py:34
  652.5 41.2 %fusion.3 = f32[32,16,256]{2,1,0:T(8,128)S(1)} fusion(f32[32,16,256,256]{3,2,1,0:T(8,128)} %get-tuple-element.14, f32[32,16,256]{2,1,0:T(8,128)S(1)} %get-tuple-element.13, pred[32,256]{1,0:T(8,128)(4,1)S(1)} %copy-done.3), kind=kLoop, calls=%fused_computation.13 | loop fusion | flops 134086656 | bytes 135274496 | tf_op jit(solution)/shard_map/reduce_sum | solution.py:36
  693.7 68.3 %fusion.57 = (f32[32,256]{1,0:T(8,128)S(1)}, bf16[32,256,1024]{2,1,0:T(8,128)(2,1)}) fusion(bf16[2,16,64,1024]{3,2,1,0:T(8,128)(2,1)} %param.25, bf16[32,256,16,64]{1,3,2,0:T(8,128)(2,1)} %bitcast.586, f32[32,16,256]{2,1,0:T(8,128)S(1)} %fusion.3, f32[32,16,256]{2,1,0:T(8,128)S(1)} %get-tuple-element.13, f32[32,16,256,256]{3,2,1,0:T(8,128)} %get-tuple-element.14, ...), kind=kOutput, calls=%fused_computation.91 | convolution fusion | flops 21701320704 | bytes 187736064 | tf_op jit(solution)/shard_map/bkrsh,krhd->bsd/dot_general | solution.py:39
  762.0 73.3 %fusion.19.clone.1.clone.5 = bf16[32,256,2816]{2,1,0:T(8,128)(2,1)} fusion(bf16[32,256,1024]{2,1,0:T(8,128)(2,1)} %get-tuple-element.16, f32[32,256]{1,0:T(8,128)S(1)} %add_rsqrt_fusion.1, bf16[2,1024,2816]{2,1,0:T(8,128)(2,1)} %param.26), kind=kOutput, calls=%fused_computation.29.clone.clone.clone.clone.clone.2 | convolution fusion | flops 47477424128 | bytes 68714496 | tf_op jit(solution)/shard_map/dot_general | solution.py:44
  835.3 56.9 %fusion.46 = (f32[32,256]{1,0:T(8,128)S(1)}, bf16[32,256,1024]{2,1,0:T(8,128)(2,1)}) fusion(bf16[2,2816,1024]{2,1,0:T(8,128)(2,1)} %param.27, bf16[32,256,1024]{2,1,0:T(8,128)(2,1)} %get-tuple-element.16, bf16[32,256,2816]{2,1,0:T(8,128)(2,1)} %fusion.19.clone.1.clone.5), kind=kOutput, calls=%fused_computation.80 | convolution fusion | flops 47294963712 | bytes 85491712 | tf_op jit(solution)/shard_map/dot_general | solution.py:45
  892.3 24.1 fusion.146
  916.5 25.0 %fusion.149 = bf16[32,256,1024]{2,1,0:T(8,128)(2,1)} fusion(bf16[32,256,1024]{2,1,0:T(8,128)(2,1)} %get-tuple-element.18, f32[32,256]{1,0:T(8,128)S(1)} %add_rsqrt_fusion, bf16[2,1024,1024]{2,1,0:T(8,128)(2,1)} %param.34), kind=kOutput, calls=%fused_computation.173 | convolution fusion | flops 17213423616 | bytes 35684352 | tf_op jit(solution)/shard_map/dot_general | solution.py:14
  943.4 24.7 %fusion.152 = bf16[32,256,1024]{2,1,0:T(8,128)(2,1)} fusion(bf16[32,256,1024]{2,1,0:T(8,128)(2,1)} %get-tuple-element.18, f32[32,256]{1,0:T(8,128)S(1)} %add_rsqrt_fusion, bf16[2,1024,1024]{2,1,0:T(8,128)(2,1)} %param.33), kind=kOutput, calls=%fused_computation.174 | convolution fusion | flops 17213423616 | bytes 35684352 | tf_op jit(solution)/shard_map/dot_general | solution.py:14
  968.3 24.9 %fusion.155 = bf16[32,256,1024]{2,1,0:T(8,128)(2,1)} fusion(bf16[32,256,1024]{2,1,0:T(8,128)(2,1)} %get-tuple-element.18, f32[32,256]{1,0:T(8,128)S(1)} %add_rsqrt_fusion, bf16[2,1024,1024]{2,1,0:T(8,128)(2,1)} %param.34), kind=kOutput, calls=%fused_computation.175 | convolution fusion | flops 17213423616 | bytes 35684352 | tf_op jit(solution)/shard_map/dot_general | solution.py:14
  1039.3 14.5 fusion.68
  1087.9 22.1 fusion.109
  1136.1 143.3 %collective-permute-done.1 = bf16[32,256,1024]{2,1,0:T(8,128)(2,1)} collective-permute-done((bf16[32,256,1024]{2,1,0:T(8,128)(2,1)}, bf16[32,256,1024]{2,1,0:T(8,128)(2,1)}, u32[]{:S(2)}, u32[]{:S(2)}) %collective-permute-start.1) | collective-permute-done | bytes 16777248 | tf_op jit(solution)/shard_map/ppermute | solution.py:84
  1279.5 22.5 copy.41
  1301.9 27.4 %bitcast_reduce_fusion.3 = (f32[32,16,96]{2,1,0:T(8,128)S(1)}, f32[32,16,256,96]{2,3,1,0:T(8,128)}) fusion(pred[32,256]{1,0:T(8,128)(4,1)S(1)} %iota_compare_fusion.2, bf16[32,256,16,64]{1,3,2,0:T(8,128)(2,1)} %bitcast.574, bf16[32,96,16,64]{1,3,2,0:T(8,128)(2,1)} %bitcast.584), kind=kOutput, calls=%fused_computation.43 | convolution fusion | flops 1648312320 | bytes 73605120 | tf_op jit(solution)/shard_map/bskrh,btkh->bkrst/dot_general | solution.py:34
  1329.4 21.8 fusion.28
  1351.1 287.8 %collective-permute-done.2 = bf16[32,256,1024]{2,1,0:T(8,128)(2,1)} collective-permute-done((bf16[32,256,1024]{2,1,0:T(8,128)(2,1)}, bf16[32,256,1024]{2,1,0:T(8,128)(2,1)}, u32[]{:S(2)}, u32[]{:S(2)}) %collective-permute-start.2) | collective-permute-done | bytes 16777248 | tf_op jit(solution)/shard_map/ppermute | solution.py:84
  1639.0 22.5 copy.43
  1661.5 30.2 %fusion.112 = (f32[32,96]{1,0:T(8,128)S(1)}, bf16[32,96,1024]{2,1,0:T(8,128)(2,1)}) fusion(bf16[32,256,16,64]{1,3,2,0:T(8,128)(2,1)} %bitcast.589, f32[32,16,96]{2,1,0:T(8,128)S(1)} %fusion.28, f32[32,16,96]{2,1,0:T(8,128)S(1)} %get-tuple-element.21, f32[32,16,256,96]{2,3,1,0:T(8,128)} %get-tuple-element.22, pred[32,256]{1,0:T(8,128)(4,1)S(1)} %iota_compare_fusion.2, ...), kind=kOutput, calls=%fused_computation.150 | convolution fusion | flops 8137995264 | bytes 82202624 | tf_op jit(solution)/shard_map/bkrsh,krhd->bsd/dot_general | solution.py:39
  1691.7 28.7 %fusion.253.clone.5 = bf16[32,96,2816]{2,1,0:T(8,128)(2,1)} fusion(bf16[32,96,1024]{2,1,0:T(8,128)(2,1)} %get-tuple-element.24, f32[32,96]{1,0:T(8,128)S(1)} %add_rsqrt_fusion.8, bf16[2,1024,2816]{2,1,0:T(8,128)(2,1)} %param.36), kind=kOutput, calls=%fused_computation.71.clone.clone.clone.clone.clone.clone.2 | convolution fusion | flops 17804034048 | bytes 29372416 | tf_op jit(solution)/shard_map/dot_general | solution.py:44
  1720.4 22.0 fusion.115
  1808.5 14.5 fusion.69
  1835.3 21.9 fusion.118
  1879.1 119.4 %collective-permute-done.3 = bf16[32,256,1024]{2,1,0:T(8,128)(2,1)} collective-permute-done((bf16[32,256,1024]{2,1,0:T(8,128)(2,1)}, bf16[32,256,1024]{2,1,0:T(8,128)(2,1)}, u32[]{:S(2)}, u32[]{:S(2)}) %collective-permute-start.3) | collective-permute-done | bytes 16777248 | tf_op jit(solution)/shard_map/ppermute | solution.py:84
  1998.5 22.4 copy.47
  2021.0 27.5 %bitcast_reduce_fusion.2 = (f32[32,16,96]{2,1,0:T(8,128)S(1)}, f32[32,16,256,96]{2,3,1,0:T(8,128)}) fusion(pred[32,256]{1,0:T(8,128)(4,1)S(1)} %copy-done.7, bf16[32,256,16,64]{1,3,2,0:T(8,128)(2,1)} %bitcast.575, bf16[32,96,16,64]{1,3,2,0:T(8,128)(2,1)} %bitcast.585), kind=kOutput, calls=%fused_computation.39 | convolution fusion | flops 1648312320 | bytes 73605120 | tf_op jit(solution)/shard_map/bskrh,btkh->bkrst/dot_general | solution.py:34
  2048.4 21.8 fusion.29
  2070.2 286.4 %collective-permute-done.4 = bf16[32,256,1024]{2,1,0:T(8,128)(2,1)} collective-permute-done((bf16[32,256,1024]{2,1,0:T(8,128)(2,1)}, bf16[32,256,1024]{2,1,0:T(8,128)(2,1)}, u32[]{:S(2)}, u32[]{:S(2)}) %collective-permute-start.4) | collective-permute-done | bytes 16777248 | tf_op jit(solution)/shard_map/ppermute | solution.py:84
  2356.6 22.4 copy.49
  2379.1 30.2 %fusion.121 = (f32[32,96]{1,0:T(8,128)S(1)}, bf16[32,96,1024]{2,1,0:T(8,128)(2,1)}) fusion(bf16[32,256,16,64]{1,3,2,0:T(8,128)(2,1)} %bitcast.588, f32[32,16,96]{2,1,0:T(8,128)S(1)} %fusion.29, f32[32,16,96]{2,1,0:T(8,128)S(1)} %get-tuple-element.31, f32[32,16,256,96]{2,3,1,0:T(8,128)} %get-tuple-element.32, pred[32,256]{1,0:T(8,128)(4,1)S(1)} %copy-done.7, ...), kind=kOutput, calls=%fused_computation.159 | convolution fusion | flops 8137995264 | bytes 82202624 | tf_op jit(solution)/shard_map/bkrsh,krhd->bsd/dot_general | solution.py:39
  2409.3 28.8 %fusion.503 = bf16[32,96,2816]{2,1,0:T(8,128)(2,1)} fusion(bf16[32,96,1024]{2,1,0:T(8,128)(2,1)} %get-tuple-element.34, f32[32,96]{1,0:T(8,128)S(1)} %add_rsqrt_fusion.5, bf16[2,1024,2816]{2,1,0:T(8,128)(2,1)} %param.36), kind=kOutput, calls=%fused_computation.79.clone.clone.clone.clone.2 | convolution fusion | flops 17804034048 | bytes 29372416 | tf_op jit(solution)/shard_map/dot_general | solution.py:44
  2438.0 23.0 fusion.123
  (81 shorter events, 220.7 us)
Async XLA Ops:
  0.0 11.9 copy-start.11
  0.0 1135.5 %collective-permute-start = (s32[32]{0:T(128)}, s32[32]{0:T(128)}, u32[]{:S(2)}, u32[]{:S(2)}) collective-permute-start(s32[32]{0:T(128)} %param.20), channel_id=1, source_target_pairs={{0,2},{1,3},{2,0},{3,1},{4,6},{5,7},{6,4},{7,5}} | collective-permute-start | bytes 392 | tf_op jit(solution)/shard_map/ppermute | solution.py:84
  130.5 22.5 copy-start.2
  395.5 56.9 %copy-start.10 = (bf16[2,1024,1024]{2,1,0:T(8,128)(2,1)S(1)}, bf16[2,1024,1024]{2,1,0:T(8,128)(2,1)}, u32[]{:S(2)}) copy-start(bf16[2,1024,1024]{2,1,0:T(8,128)(2,1)} %param.22) | copy-start | bytes 12582916
  452.5 24.2 copy-start.12
  476.7 24.4 copy-start.13
  570.5 22.5 copy-start.3
  835.3 57.0 %copy-start.14 = (bf16[2,1024,1024]{2,1,0:T(8,128)(2,1)S(1)}, bf16[2,1024,1024]{2,1,0:T(8,128)(2,1)}, u32[]{:S(2)}) copy-start(bf16[2,1024,1024]{2,1,0:T(8,128)(2,1)} %param.33) | copy-start | bytes 12582916
  916.4 363.1 %collective-permute-start.1 = (bf16[32,256,1024]{2,1,0:T(8,128)(2,1)}, bf16[32,256,1024]{2,1,0:T(8,128)(2,1)}, u32[]{:S(2)}, u32[]{:S(2)}) collective-permute-start(bf16[32,256,1024]{2,1,0:T(8,128)(2,1)} %fusion.146), channel_id=1, source_target_pairs={{0,2},{1,3},{2,0},{3,1},{4,6},{5,7},{6,4},{7,5}} | collective-permute-start | bytes 50331656 | tf_op jit(solution)/shard_map/ppermute | solution.py:84
  941.5 697.5 %collective-permute-start.2 = (bf16[32,256,1024]{2,1,0:T(8,128)(2,1)}, bf16[32,256,1024]{2,1,0:T(8,128)(2,1)}, u32[]{:S(2)}, u32[]{:S(2)}) collective-permute-start(bf16[32,256,1024]{2,1,0:T(8,128)(2,1)} %fusion.149), channel_id=1, source_target_pairs={{0,2},{1,3},{2,0},{3,1},{4,6},{5,7},{6,4},{7,5}} | collective-permute-start | bytes 50331656 | tf_op jit(solution)/shard_map/ppermute | solution.py:84
  943.4 51.5 %slice-start = ((s8[6291456]{0:T(1024)(128)(4,1)}), s8[4194304]{0:T(1024)(128)(4,1)S(1)}, s32[]{:S(2)}) async-start(s8[6291456]{0:T(1024)(128)(4,1)} %bitcast.592), calls=%async_computation | async-start | bytes 8388608
  968.1 26.8 %slice-start.1 = ((s8[6291456]{0:T(1024)(128)(4,1)}), s8[2097152]{0:T(1024)(128)(4,1)S(1)}, s32[]{:S(2)}) async-start(s8[6291456]{0:T(1024)(128)(4,1)} %bitcast.592), calls=%async_computation.1 | async-start | bytes 4194304
  968.1 1030.4 %collective-permute-start.3 = (bf16[32,256,1024]{2,1,0:T(8,128)(2,1)}, bf16[32,256,1024]{2,1,0:T(8,128)(2,1)}, u32[]{:S(2)}, u32[]{:S(2)}) collective-permute-start(bf16[32,256,1024]{2,1,0:T(8,128)(2,1)} %fusion.152), channel_id=1, source_target_pairs={{0,2},{1,3},{2,0},{3,1},{4,6},{5,7},{6,4},{7,5}} | collective-permute-start | bytes 50331656 | tf_op jit(solution)/shard_map/ppermute | solution.py:84
  993.2 1363.4 %collective-permute-start.4 = (bf16[32,256,1024]{2,1,0:T(8,128)(2,1)}, bf16[32,256,1024]{2,1,0:T(8,128)(2,1)}, u32[]{:S(2)}, u32[]{:S(2)}) collective-permute-start(bf16[32,256,1024]{2,1,0:T(8,128)(2,1)} %fusion.155), channel_id=1, source_target_pairs={{0,2},{1,3},{2,0},{3,1},{4,6},{5,7},{6,4},{7,5}} | collective-permute-start | bytes 50331656 | tf_op jit(solution)/shard_map/ppermute | solution.py:84
  1039.3 48.6 %copy-start.4 = (pred[96,96]{0,1:T(8,128)(4,1)}, pred[96,96]{0,1:T(8,128)(4,1)S(1)}, u32[]{:S(2)}) copy-start(pred[96,96]{0,1:T(8,128)(4,1)S(1)} %iota_compare_fusion) | copy-start | bytes 27652
  1111.9 11.5 copy-start
  1136.1 525.3 %copy-start.6 = (pred[32,256]{1,0:T(8,128)(4,1)}, pred[32,256]{1,0:T(8,128)(4,1)S(1)}, u32[]{:S(2)}) copy-start(pred[32,256]{1,0:T(8,128)(4,1)S(1)} %iota_compare_fusion.2) | copy-start | bytes 24580
  1691.6 28.7 %copy-start.8 = (bf16[2,2816,1024]{2,1,0:T(8,128)(2,1)S(1)}, bf16[2,2816,1024]{2,1,0:T(8,128)(2,1)}, u32[]{:S(2)}) copy-start(bf16[2,2816,1024]{2,1,0:T(8,128)(2,1)} %param.37) | copy-start | bytes 34603012
  1720.4 24.8 %copy-start.15 = (bf16[2,1024,1024]{2,1,0:T(8,128)(2,1)S(1)}, bf16[2,1024,1024]{2,1,0:T(8,128)(2,1)}, u32[]{:S(2)}) copy-start(bf16[2,1024,1024]{2,1,0:T(8,128)(2,1)} %param.28) | copy-start | bytes 12582916
  1742.4 2.7 copy-start.16
  1786.7 21.9 copy-start.5
  1879.1 141.8 %copy-start.7 = (pred[32,256]{1,0:T(8,128)(4,1)S(1)}, pred[32,256]{1,0:T(8,128)(4,1)}, u32[]{:S(2)}) copy-start(pred[32,256]{1,0:T(8,128)(4,1)} %copy-done.6) | copy-start | bytes 24580
  2070.2 308.9 %copy-start.1 = (bf16[16,64,1024,1]{2,1,0,3:T(8,128)(2,1)S(1)}, bf16[16,64,1024,1]{2,1,0,3:T(8,128)(2,1)}, u32[]{:S(2)}) copy-start(bf16[16,64,1024,1]{2,1,0,3:T(8,128)(2,1)} %fusion.298.clone.5) | copy-start | bytes 6291460
  2409.2 28.8 %copy-start.9 = (bf16[2,2816,1024]{2,1,0:T(8,128)(2,1)S(1)}, bf16[2,2816,1024]{2,1,0:T(8,128)(2,1)}, u32[]{:S(2)}) copy-start(bf16[2,2816,1024]{2,1,0:T(8,128)(2,1)} %param.37) | copy-start | bytes 34603012
where the time goes:
time: 2470 us; the launch traced here: 2460 us
  matrix products  1140 us (46%)
  waiting for transfers between devices  837 us (34%)
  local copies, waits for them, and re-layouts  316 us (13%)
  other arithmetic  161 us (7%)
    ppermute x5, waiting for transfers between devices, per_device(): lax.ppermute((own_keys, own_vals, enc_len), 'pair', to_partner)  837 us
    dot_general x18, matrix products, project(): jnp.dot(source, weight, preferred_element_type=jnp.float32)  332 us
    dot_general x6, matrix products, attend(): jnp.einsum('bkrsh,krhd->bsd', context, w_out, preferred_element_type=jnp....  241 us
    convert_element_type x14, local copies, waits for them, and re-layouts, project(): jnp.dot(source, weight, preferred_element_type=jnp.float32)  220 us
    dot_general x4, matrix products, feed_forward(): jnp.dot(normed, w_up, preferred_element_type=jnp.float32)  204 us
    dot_general x6, matrix products, attend(): jnp.einsum('bskrh,btkh->bkrst', q_heads, k_heads, preferred_element_type=...  203 us
    dot_general x4, matrix products, feed_forward(): jnp.dot(inner_act, w_down, preferred_element_type=jnp.float32)  159 us
    reduce_sum x6, other arithmetic, attend(): attn_probs = jax.nn.softmax(scores, axis=-1).astype(jnp.bfloat16)  150 us
  transfers between devices with their start and end apart: 5, of which 4 were waited for; matrix products, arithmetic and copies ran while one was open for 61% of the time, Pallas kernels for 0%

commit v1 on v0

v1 whole, which is shorter than its diff:
```python
import functools

import jax
import jax.numpy as jnp
from jax import lax
from jax.experimental import pallas as pl
from jax.experimental.pallas import tpu as pltpu
from jax.sharding import PartitionSpec as P

BF16 = jnp.bfloat16
F32 = jnp.float32
I32 = jnp.int32

ROWS = 32
T_ENC = 256
T_DEC = 96
D = 1024
FF = 2816
PAIRS = 8
BIN = 512
NB = ROWS * T_ENC // BIN
CHUNKS = 4
CB = NB // CHUNKS
UNIT = 16
SCALE = 64 ** -0.5 * 1.4426950408889634
VMEM_MAX = 64 * 2**20 - 2**17

P_ORDER, P_OFF, P_LEN, P_GLOB, P_START, P_NBINS = 0, 32, 64, 96, 128, 160


def plan_kernel(len_ref, plan_ref, free, count, rbin, roff, rk):
    def clear(i, _):
        free[i] = BIN // UNIT
        count[i] = 0
        return 0

    lax.fori_loop(0, NB + 1, clear, 0)

    def by_size(i, nbins):
        size = T_ENC // UNIT - i

        def by_row(r, nbins):
            hit = (len_ref[r] + UNIT - 1) // UNIT == size

            @pl.when(hit)
            def _():
                b = lax.while_loop(lambda b: free[b] < size, lambda b: b + 1, jnp.int32(0))
                left = free[b]
                rbin[r] = b
                roff[r] = BIN - left * UNIT
                rk[r] = count[b]
                free[b] = left - size
                count[b] = count[b] + 1

            return nbins

        return lax.fori_loop(0, ROWS, by_row, nbins)

    lax.fori_loop(0, T_ENC // UNIT, by_size, 0)

    def starts(b, carry):
        total, nbins = carry
        plan_ref[P_START + b] = total
        c = count[b]
        return total + c, nbins + jnp.where(c > 0, 1, 0)

    total, nbins = lax.fori_loop(0, NB, starts, (jnp.int32(0), jnp.int32(0)))
    plan_ref[P_START + NB] = total

    def fill(i, _):
        plan_ref[i] = nbins
        return 0

    lax.fori_loop(P_START + NB + 1, 256, fill, 0)

    def place(r, _):
        b = rbin[r]
        pos = plan_ref[P_START + b] + rk[r]
        plan_ref[P_ORDER + pos] = r
        plan_ref[P_OFF + pos] = roff[r]
        plan_ref[P_LEN + pos] = len_ref[r]
        plan_ref[P_GLOB + pos] = b * BIN + roff[r]
        return 0

    lax.fori_loop(0, ROWS, place, 0)


def make_plan(enc_len):
    smem = pl.BlockSpec(memory_space=pltpu.SMEM)
    return pl.pallas_call(
        plan_kernel,
        out_shape=jax.ShapeDtypeStruct((256,), I32),
        in_specs=[smem],
        out_specs=smem,
        scratch_shapes=[pltpu.SMEM((32,), I32) for _ in range(5)],
        name="plan",
    )(enc_len)


def norm_rows(src, dst, rows, step=128):
    for m in range(0, rows, step):
        v = src[m:m + step, :].astype(F32)
        inv = lax.rsqrt(jnp.mean(v * v, axis=-1, keepdims=True) + 1e-6)
        dst[m:m + step, :] = (v * inv).astype(BF16)


def gelu(x):
    inner = x * (x * x * (0.044715 * 0.7978845608028654) + 0.7978845608028654)
    half = x * 0.5
    return half + half * jnp.tanh(inner)


def attend_pair(q, k, v, mask, vmask=None):
    tq, tk = q.shape[0], k.shape[0]
    lane = lax.broadcasted_iota(I32, (tq, 128), 1)
    low = (lane < 64)
    lowf = low.astype(F32).astype(BF16)
    q2 = jnp.concatenate([q * lowf, q * (1 - lowf)], axis=0)
    s = lax.dot_general(q2, k, (((1,), (1,)), ((), ())), preferred_element_type=F32)
    s = jnp.where(mask, s, -1e30)
    top = jnp.max(s, axis=-1, keepdims=True)
    e = jnp.exp2((s - top) * SCALE).astype(BF16)
    if vmask is not None:
        v = jnp.where(vmask, v, jnp.zeros_like(v))
    va = jnp.concatenate([v, jnp.ones_like(v)], axis=1)
    o = jnp.dot(e, va, preferred_element_type=F32)
    num = jnp.where(low, o[:tq, :128], o[tq:, :128])
    den = jnp.where(low, o[:tq, 128:], o[tq:, 128:])
    return (num / den).astype(BF16)


def enc_kernel(chunk, plan, x_hbm, wq_h, wk_h, wv_h, wo_h, w1_h, w2_h, out_ref,
               xb, n_s, q_s, k_s, v_s, c_s, inner, wq, wk, wv, wo, w1, w2, xsem, wsem):
    i = pl.program_id(0)
    b = chunk * CB + i
    nbins = plan[P_NBINS]
    slot = lax.rem(i, 2)
    weights = [(wq_h, wq), (wk_h, wk), (wv_h, wv), (wo_h, wo), (w1_h, w1), (w2_h, w2)]

    def weight_copy(j, l):
        return pltpu.make_async_copy(weights[j][0].at[l], weights[j][1].at[l], wsem.at[j, l])

    def row_copies(bb, sl, start):
        def per_row(pos, _):
            row, off = plan[P_ORDER + pos], plan[P_OFF + pos]
            units = (plan[P_LEN + pos] + UNIT - 1) // UNIT
            for bit in (16, 8, 4, 2, 1):
                @pl.when((units & bit) != 0)
                def _():
                    at = (units & ~(2 * bit - 1)) * UNIT
                    cp = pltpu.make_async_copy(
                        x_hbm.at[row, pl.ds(pl.multiple_of(at, UNIT), bit * UNIT), :],
                        xb.at[sl, pl.ds(pl.multiple_of(off + at, UNIT), bit * UNIT), :],
                        xsem.at[sl])
                    if start:
                        cp.start()
                    else:
                        cp.wait()
            return 0

        lax.fori_loop(plan[P_START + bb], plan[P_START + bb + 1], per_row, 0)

    @pl.when(jnp.logical_and(i == 0, b < nbins))
    def _():
        row_copies(b, slot, True)
        for l in range(2):
            for j in range(6):
                weight_copy(j, l).start()
        tail = slice(BIN, BIN + T_ENC)
        for ref in (q_s, k_s, v_s):
            ref[tail, :] = jnp.zeros((T_ENC, D), BF16)
        c_s[...] = jnp.zeros_like(c_s)

    @pl.when(jnp.logical_and(i + 1 < CB, b + 1 < nbins))
    def _():
        row_copies(b + 1, 1 - slot, True)

    @pl.when(b >= nbins)
    def _():
        out_ref[...] = jnp.zeros_like(out_ref)

    @pl.when(b < nbins)
    def _():
        row_copies(b, slot, False)
        first, last = plan[P_START + b], plan[P_START + b + 1]
        used = plan[P_OFF + last - 1] + (plan[P_LEN + last - 1] + UNIT - 1) // UNIT * UNIT
        h = xb.at[slot]

        def zero_unit(u, _):
            h[pl.ds(pl.multiple_of(u * UNIT, UNIT), UNIT), :] = jnp.zeros((UNIT, D), BF16)
            return 0

        lax.fori_loop(used // UNIT, BIN // UNIT, zero_unit, 0)

        def need(j, l):
            @pl.when(i == 0)
            def _():
                weight_copy(j, l).wait()

        def layer(l, _):
            for j in range(3):
                need(j, l)
            norm_rows(h, n_s, BIN)
            for w, dst in ((wq, q_s), (wk, k_s), (wv, v_s)):
                for n in range(0, D, 256):
                    dst[0:BIN, n:n + 256] = jnp.dot(n_s[...], w[l, :, n:n + 256], preferred_element_type=F32).astype(BF16)

            def per_row(pos, _):
                off = pl.multiple_of(plan[P_OFF + pos], UNIT)
                length = plan[P_LEN + pos]

                def run(t):
                    mask = lax.broadcasted_iota(I32, (2 * t, t), 1) < length
                    rows = pl.ds(off, t)

                    def pair(p, _):
                        cols = pl.ds(pl.multiple_of(p * 128, 128), 128)
                        c_s[rows, cols] = attend_pair(q_s[rows, cols], k_s[rows, cols], v_s[rows, cols], mask)
                        return 0

                    lax.fori_loop(0, PAIRS, pair, 0, unroll=2)

                for lo, t in ((0, 128), (128, 192), (192, 256)):
                    @pl.when(jnp.logical_and(length > lo, length <= t))
                    def _():
                        run(t)

                return 0

            lax.fori_loop(first, last, per_row, 0)
            need(3, l)
            need(4, l)
            for n in range(0, D, 256):
                u = jnp.dot(c_s[0:BIN, :], wo[l, :, n:n + 256], preferred_element_type=F32)
                h[:, n:n + 256] = (h[:, n:n + 256].astype(F32) + u).astype(BF16)
            norm_rows(h, n_s, BIN)
            for n in range(0, FF, 256):
                u = jnp.dot(n_s[...], w1[l, :, n:n + 256], preferred_element_type=F32)
                inner[:, n:n + 256] = gelu(u).astype(BF16)
            need(5, l)
            for n in range(0, D, 256):
                u = jnp.dot(inner[...], w2[l, :, n:n + 256], preferred_element_type=F32)
                h[:, n:n + 256] = (h[:, n:n + 256].astype(F32) + u).astype(BF16)
            return 0

        lax.fori_loop(0, 2, layer, 0)
        norm_rows(h, out_ref, BIN)


def encode_chunk(chunk, plan, x_enc, weights):
    hbm = pl.BlockSpec(memory_space=pl.ANY)
    vm = lambda *s: pltpu.VMEM(s, BF16)
    tokens = BIN + T_ENC
    return pl.pallas_call(
        functools.partial(enc_kernel, chunk),
        out_shape=jax.ShapeDtypeStruct((CB * BIN, D), BF16),
        grid_spec=pltpu.PrefetchScalarGridSpec(
            num_scalar_prefetch=1,
            grid=(CB,),
            in_specs=[hbm] * 7,
            out_specs=pl.BlockSpec((BIN, D), lambda i, plan: (i, 0)),
            scratch_shapes=[
                vm(2, BIN, D), vm(BIN, D), vm(tokens, D), vm(tokens, D), vm(tokens, D), vm(tokens, D), vm(BIN, FF),
                vm(2, D, D), vm(2, D, D), vm(2, D, D), vm(2, D, D), vm(2, D, FF), vm(2, FF, D),
                pltpu.SemaphoreType.DMA((2,)), pltpu.SemaphoreType.DMA((6, 2)),
            ],
        ),
        compiler_params=pltpu.CompilerParams(vmem_limit_bytes=VMEM_MAX, dimension_semantics=("arbitrary",)),
        cost_estimate=pl.CostEstimate(flops=80_000_000_000, bytes_accessed=60_000_000, transcendentals=0),
        name="encode",
    )(plan, x_enc, *weights)


def cross_kernel(base, plan, h_ref, wk_ref, wv_ref, k0_ref, v0_ref, k1_ref, v1_ref):
    @pl.when(base + pl.program_id(0) < plan[P_NBINS])
    def _():
        for l, k_ref, v_ref in ((0, k0_ref, v0_ref), (1, k1_ref, v1_ref)):
            for w, dst in ((wk_ref, k_ref), (wv_ref, v_ref)):
                for n in range(0, D, 256):
                    dst[:, n:n + 256] = jnp.dot(h_ref[...], w[l, :, n:n + 256], preferred_element_type=F32).astype(BF16)


def cross_keys(base, plan, h, wk, wv):
    tokens = h.shape[0]
    whole = pl.BlockSpec((2, D, D), lambda i, plan: (0, 0, 0))

    def block(i, plan):
        return jnp.minimum(i, jnp.maximum(plan[P_NBINS] - 1 - base, 0)), 0

    spec = pl.BlockSpec((BIN, D), block)
    return pl.pallas_call(
        functools.partial(cross_kernel, base),
        out_shape=[jax.ShapeDtypeStruct((tokens, D), BF16)] * 4,
        grid_spec=pltpu.PrefetchScalarGridSpec(
            num_scalar_prefetch=1, grid=(tokens // BIN,), in_specs=[spec, whole, whole], out_specs=[spec] * 4),
        compiler_params=pltpu.CompilerParams(vmem_limit_bytes=VMEM_MAX, dimension_semantics=("arbitrary",)),
        cost_estimate=pl.CostEstimate(flops=8 * tokens * D * D, bytes_accessed=10 * tokens * D, transcendentals=0),
        name="cross_keys",
    )(plan, h, wk, wv)


G = 4
MG = G * T_DEC
HALF = ROWS // 2
HALF_TOKENS = NB * BIN // 2


def dec_kernel(half, plan, *refs):
    nkv = half + 1
    y_hbm = refs[0]
    kv_hbm = refs[1:1 + 4 * nkv]
    w_hbm = refs[1 + 4 * nkv:9 + 4 * nkv]
    rest = refs[9 + 4 * nkv + (1 if half else 0):]
    out_hbm, zb, n_s, q_s, k_s, v_s, c_s, inner, kb, vb = rest[:10]
    w_s = rest[10:18]
    ysem, osem, kvsem, wsem = rest[18:]
    wq, wk, wv, wo, cq, co, w1, w2 = w_s
    i = pl.program_id(0)
    groups = pl.num_programs(0)
    slot = lax.rem(i, 2)

    def weight_copy(j, l):
        return pltpu.make_async_copy(w_hbm[j].at[l], w_s[j].at[l], wsem.at[j, l])

    def first_row(g):
        return half * HALF + g * G

    def y_copy(g, sl, r):
        row = plan[P_ORDER + first_row(g) + r]
        return pltpu.make_async_copy(y_hbm.at[row], zb.at[sl, pl.ds(r * T_DEC, T_DEC), :], ysem.at[sl])

    def out_copy(g, sl, r):
        row = plan[P_ORDER + first_row(g) + r]
        return pltpu.make_async_copy(zb.at[sl, pl.ds(r * T_DEC, T_DEC), :], out_hbm.at[row], osem.at[sl])

    def kv_copies(l, start):
        def per_row(r, _):
            pos = first_row(i) + r
            at_glob = plan[P_GLOB + pos]
            units = (plan[P_LEN + pos] + UNIT - 1) // UNIT
            for part in range(nkv):
                for which, dst in ((0, kb), (1, vb)):
                    src = (kv_hbm[4 * part + which], kv_hbm[4 * part + 2 + which])

                    for bit in (16, 8, 4, 2, 1):
                        inside = jnp.logical_and(at_glob >= part * HALF_TOKENS, at_glob < (part + 1) * HALF_TOKENS)

                        @pl.when(jnp.logical_and(inside, (units & bit) != 0))
                        def _():
                            at = (units & ~(2 * bit - 1)) * UNIT
                            cp = pltpu.make_async_copy(
                                src[l].at[pl.ds(pl.multiple_of(at_glob - part * HALF_TOKENS + at, UNIT), bit * UNIT), :],
                                dst.at[r, pl.ds(pl.multiple_of(at, UNIT), bit * UNIT), :],
                                kvsem)
                            if start:
                                cp.start()
                            else:
                                cp.wait()
            return 0

        lax.fori_loop(0, G, per_row, 0)

    @pl.when(i == 0)
    def _():
        for r in range(G):
            y_copy(0, 0, r).start()
        for l in range(2):
            for j in range(8):
                weight_copy(j, l).start()

    @pl.when(i >= 1)
    def _():
        for r in range(G):
            out_copy(i - 1, 1 - slot, r).wait()

    @pl.when(i + 1 < groups)
    def _():
        for r in range(G):
            y_copy(i + 1, 1 - slot, r).start()

    for r in range(G):
        y_copy(i, slot, r).wait()
    z = zb.at[slot]

    def need(j, l):
        @pl.when(i == 0)
        def _():
            weight_copy(j, l).wait()

    def add_to_z(src, w, l):
        for n in range(0, D, 256):
            u = jnp.dot(src[...], w[l, :, n:n + 256], preferred_element_type=F32)
            z[:, n:n + 256] = (z[:, n:n + 256].astype(F32) + u).astype(BF16)

    for l in range(2):
        kv_copies(l, True)
        for j in range(3):
            need(j, l)
        norm_rows(z, n_s, MG)
        for w, dst in ((wq, q_s), (wk, k_s), (wv, v_s)):
            for n in range(0, D, 256):
                dst[:, n:n + 256] = jnp.dot(n_s[...], w[l, :, n:n + 256], preferred_element_type=F32).astype(BF16)
        row_at = lax.broadcasted_iota(I32, (2 * T_DEC, T_DEC), 0)
        row_at = jnp.where(row_at >= T_DEC, row_at - T_DEC, row_at)
        causal = row_at >= lax.broadcasted_iota(I32, (2 * T_DEC, T_DEC), 1)

        def self_pair(p, _):
            cols = pl.ds(pl.multiple_of(p * 128, 128), 128)
            for r in range(G):
                rows = slice(r * T_DEC, (r + 1) * T_DEC)
                c_s[rows, cols] = attend_pair(q_s[rows, cols], k_s[rows, cols], v_s[rows, cols], causal)
            return 0

        lax.fori_loop(0, PAIRS, self_pair, 0)
        need(3, l)
        need(4, l)
        add_to_z(c_s, wo, l)
        norm_rows(z, n_s, MG)
        for n in range(0, D, 256):
            q_s[:, n:n + 256] = jnp.dot(n_s[...], cq[l, :, n:n + 256], preferred_element_type=F32).astype(BF16)
        kv_copies(l, False)

        def cross_pair(p, _):
            cols = pl.ds(pl.multiple_of(p * 128, 128), 128)
            for r in range(G):
                length = plan[P_LEN + first_row(i) + r]
                mask = lax.broadcasted_iota(I32, (2 * T_DEC, T_ENC), 1) < length
                vmask = lax.broadcasted_iota(I32, (T_ENC, 128), 0) < length
                rows = slice(r * T_DEC, (r + 1) * T_DEC)
                c_s[rows, cols] = attend_pair(q_s[rows, cols], kb[r, :, cols], vb[r, :, cols], mask, vmask)
            return 0

        lax.fori_loop(0, PAIRS, cross_pair, 0)
        need(5, l)
        need(6, l)
        add_to_z(c_s, co, l)
        norm_rows(z, n_s, MG)
        for n in range(0, FF, 256):
            u = jnp.dot(n_s[...], w1[l, :, n:n + 256], preferred_element_type=F32)
            inner[:, n:n + 256] = gelu(u).astype(BF16)
        need(7, l)
        add_to_z(inner, w2, l)

    for r in range(G):
        out_copy(i, slot, r).start()

    @pl.when(i == groups - 1)
    def _():
        for r in range(G):
            out_copy(i, slot, r).wait()


def decode_half(half, plan, y_dec, kvs, weights, prev):
    hbm = pl.BlockSpec(memory_space=pl.ANY)
    vm = lambda *s: pltpu.VMEM(s, BF16)
    ins = [y_dec, *kvs, *weights] + ([prev] if half else [])
    return pl.pallas_call(
        functools.partial(dec_kernel, half),
        out_shape=jax.ShapeDtypeStruct((ROWS, T_DEC, D), BF16),
        grid_spec=pltpu.PrefetchScalarGridSpec(
            num_scalar_prefetch=1,
            grid=(HALF // G,),
            in_specs=[hbm] * len(ins),
            out_specs=hbm,
            scratch_shapes=[
                vm(2, MG, D), vm(MG, D), vm(MG, D), vm(MG, D), vm(MG, D), vm(MG, D), vm(MG, FF),
                vm(G, T_ENC, D), vm(G, T_ENC, D),
                vm(2, D, D), vm(2, D, D), vm(2, D, D), vm(2, D, D), vm(2, D, D), vm(2, D, D), vm(2, D, FF), vm(2, FF, D),
                pltpu.SemaphoreType.DMA((2,)), pltpu.SemaphoreType.DMA((2,)), pltpu.SemaphoreType.DMA,
                pltpu.SemaphoreType.DMA((8, 2)),
            ],
        ),
        input_output_aliases={len(ins): 0} if half else {},
        compiler_params=pltpu.CompilerParams(vmem_limit_bytes=VMEM_MAX, dimension_semantics=("arbitrary",)),
        cost_estimate=pl.CostEstimate(flops=90_000_000_000, bytes_accessed=100_000_000, transcendentals=0),
        name="decode",
    )(plan, *ins)


def solution(mesh):
    pair_size = mesh.shape["pair"]
    to_partner = [(source, (source + pair_size // 2) % pair_size) for source in range(pair_size)]
    row_spec = P(("data", "pair"))
    full_spec = P()

    def per_device(x_enc, enc_len, y_dec, enc_wq, enc_wk, enc_wv, enc_wo, enc_w1, enc_w2, dec_wq, dec_wk, dec_wv, dec_wo, crs_wq, crs_wk, crs_wv, crs_wo, dec_w1, dec_w2):
        flat = lambda w: w.reshape(2, D, D)
        plan = make_plan(enc_len)
        partner_plan = lax.ppermute(plan, "pair", to_partner)
        enc_weights = (enc_wq, enc_wk, enc_wv, flat(enc_wo), enc_w1, enc_w2)
        enc_out = []
        for chunk in range(CHUNKS):
            h = encode_chunk(chunk, plan, x_enc, enc_weights)
            enc_out.append(lax.ppermute(h, "pair", to_partner))
        dec_weights = (dec_wq, dec_wk, dec_wv, flat(dec_wo), crs_wq, flat(crs_wo), dec_w1, dec_w2)
        out, kvs = None, []
        for half in range(2):
            h = jnp.concatenate(enc_out[2 * half:2 * half + 2], axis=0)
            kvs += cross_keys(half * NB // 2, partner_plan, h, crs_wk, crs_wv)
            out = decode_half(half, partner_plan, y_dec, kvs, dec_weights, out)
        return out

    return jax.shard_map(per_device, mesh=mesh, in_specs=(row_spec, row_spec, row_spec) + (full_spec,) * 16, out_specs=row_spec, check_vma=False)
```

time: 2470 us -> 1180 us (0.48)
  the two profiles are of different devices: /device:TPU:0 before, /device:TPU:7 now
where the time goes in v1:
time: 1180 us
  Pallas kernels  952 us (81%)
  waiting for transfers between devices  161 us (14%)
  starting transfers between devices  48.1 us (4%)
  other arithmetic  15.3 us (1%)
    pallas_call x4, Pallas kernels, encode_chunk(): pl.pallas_call(functools.partial(enc_kernel, chunk), out_shape=jax.ShapeD...  467 us
    pallas_call x2, Pallas kernels, decode_half(): pl.pallas_call(functools.partial(dec_kernel, half), out_shape=jax.ShapeDt...  402 us
    ppermute x4, waiting for transfers between devices, per_device(): enc_out.append(lax.ppermute(h, 'pair', to_partner))  161 us
    pallas_call x2, Pallas kernels, cross_keys(): pl.pallas_call(functools.partial(cross_kernel, base), out_shape=[jax.Shap...  68.1 us
    ppermute x4, starting transfers between devices, per_device(): enc_out.append(lax.ppermute(h, 'pair', to_partner))  46.6 us
  transfers between devices with their start and end apart: 5, of which 2 were waited for; matrix products, arithmetic and copies ran while one was open for 1% of the time, Pallas kernels for 26%

profile of v1, /device:TPU:7, one launch (start us, length us, event | category | flops | bytes accessed | tf_op | source)
XLA Modules:
  0.0 1177.6 jit_solution(14014065678196760455)
XLA Ops:
  0.0 14.8 %plan.1 = s32[256]{0:T(256)} custom-call(s32[32]{0:T(128)} %len_ref.1), custom_call_target="tpu_custom_call" | custom-call | tf_op jit(solution)/shard_map/plan/pallas_call | solution.py:90
  14.8 155.7 %encode.4 = bf16[2048,1024]{1,0:T(8,128)(2,1)} custom-call(s32[256]{0:T(256)} %plan.1, bf16[32,256,1024]{2,1,0:T(8,128)(2,1)} %x_hbm.7, bf16[2,1024,1024]{2,1,0:T(8,128)(2,1)} %wq_h.7, bf16[2,1024,1024]{2,1,0:T(8,128)(2,1)} %wk_h.7, bf16[2,1024,1024]{2,1,0:T(8,128)(2,1)} %wv_h.7, bf16[2,1024,1024]{2,1,0:T(8,128)(2,1)} %bitcast.3, ...), custom_call_target="tpu_custom_call" | custom-call | flops 80000000000 | bytes 60000000 | tf_op jit(solution)/shard_map/encode/pallas_call | solution.py:254
  170.5 0.0 collective-permute-start.1
  170.5 182.4 %encode.5 = bf16[2048,1024]{1,0:T(8,128)(2,1)} custom-call(s32[256]{0:T(256)} %plan.1, bf16[32,256,1024]{2,1,0:T(8,128)(2,1)} %x_hbm.7, bf16[2,1024,1024]{2,1,0:T(8,128)(2,1)} %wq_h.7, bf16[2,1024,1024]{2,1,0:T(8,128)(2,1)} %wk_h.7, bf16[2,1024,1024]{2,1,0:T(8,128)(2,1)} %wv_h.7, bf16[2,1024,1024]{2,1,0:T(8,128)(2,1)} %bitcast.4, ...), custom_call_target="tpu_custom_call" | custom-call | flops 80000000000 | bytes 60000000 | tf_op jit(solution)/shard_map/encode/pallas_call | solution.py:254
  352.9 0.0 collective-permute-start.2
  353.0 122.2 %encode.6 = bf16[2048,1024]{1,0:T(8,128)(2,1)} custom-call(s32[256]{0:T(256)} %plan.1, bf16[32,256,1024]{2,1,0:T(8,128)(2,1)} %x_hbm.7, bf16[2,1024,1024]{2,1,0:T(8,128)(2,1)} %wq_h.7, bf16[2,1024,1024]{2,1,0:T(8,128)(2,1)} %wk_h.7, bf16[2,1024,1024]{2,1,0:T(8,128)(2,1)} %wv_h.7, bf16[2,1024,1024]{2,1,0:T(8,128)(2,1)} %bitcast.5, ...), custom_call_target="tpu_custom_call" | custom-call | flops 80000000000 | bytes 60000000 | tf_op jit(solution)/shard_map/encode/pallas_call | solution.py:254
  475.1 0.0 copy-start
  475.2 46.5 %collective-permute-start.3 = (bf16[2048,1024]{1,0:T(8,128)(2,1)}, bf16[2048,1024]{1,0:T(8,128)(2,1)}, u32[]{:S(2)}, u32[]{:S(2)}) collective-permute-start(bf16[2048,1024]{1,0:T(8,128)(2,1)} %encode.6), channel_id=1, source_target_pairs={{0,2},{1,3},{2,0},{3,1},{4,6},{5,7},{6,4},{7,5}} | collective-permute-start | bytes 12582920 | tf_op jit(solution)/shard_map/ppermute | solution.py:494
  521.7 7.1 encode.7
  528.8 0.0 collective-permute-start.4
  528.8 0.0 copy-done
  528.8 1.4 collective-permute-start
  530.3 0.0 collective-permute-done.1
  530.3 0.0 collective-permute-done.2
  530.3 7.7 pad_maximum_fusion.h_ref
  538.0 74.9 %collective-permute-done.3 = bf16[2048,1024]{1,0:T(8,128)(2,1)} collective-permute-done((bf16[2048,1024]{1,0:T(8,128)(2,1)}, bf16[2048,1024]{1,0:T(8,128)(2,1)}, u32[]{:S(2)}, u32[]{:S(2)}) %collective-permute-start.3) | collective-permute-done | bytes 4194336 | tf_op jit(solution)/shard_map/ppermute | solution.py:494
  612.9 85.9 %collective-permute-done.4 = bf16[2048,1024]{1,0:T(8,128)(2,1)} collective-permute-done((bf16[2048,1024]{1,0:T(8,128)(2,1)}, bf16[2048,1024]{1,0:T(8,128)(2,1)}, u32[]{:S(2)}, u32[]{:S(2)}) %collective-permute-start.4) | collective-permute-done | bytes 4194336 | tf_op jit(solution)/shard_map/ppermute | solution.py:494
  698.8 7.7 pad_maximum_fusion.1.h_ref
  706.5 0.0 collective-permute-done.plan
  706.5 0.0 copy-start.1
  706.5 0.6 copy-done.1
  707.0 25.1 %cross_keys.3 = (bf16[4096,1024]{1,0:T(8,128)(2,1)}, bf16[4096,1024]{1,0:T(8,128)(2,1)}, bf16[4096,1024]{1,0:T(8,128)(2,1)}, bf16[4096,1024]{1,0:T(8,128)(2,1)}) custom-call(s32[256]{0:T(256)} %copy-done.1, bf16[4096,1024]{1,0:T(8,128)(2,1)} %pad_maximum_fusion.1.h_ref, bf16[2,1024,1024]{2,1,0:T(8,128)(2,1)} %wk_ref.3, bf16[2,1024,1024]{2,1,0:T(8,128)(2,1)} %wv_ref.3), custom_call_target="tpu_custom_call" | custom-call | flops 34359738368 | bytes 41943040 | tf_op jit(solution)/shard_map/cross_keys/pallas_call | solution.py:291
  732.1 43.0 %cross_keys.2 = (bf16[4096,1024]{1,0:T(8,128)(2,1)}, bf16[4096,1024]{1,0:T(8,128)(2,1)}, bf16[4096,1024]{1,0:T(8,128)(2,1)}, bf16[4096,1024]{1,0:T(8,128)(2,1)}) custom-call(s32[256]{0:T(256)} %copy-done.1, bf16[4096,1024]{1,0:T(8,128)(2,1)} %pad_maximum_fusion.h_ref, bf16[2,1024,1024]{2,1,0:T(8,128)(2,1)} %wk_ref.3, bf16[2,1024,1024]{2,1,0:T(8,128)(2,1)} %wv_ref.3), custom_call_target="tpu_custom_call" | custom-call | flops 34359738368 | bytes 41943040 | tf_op jit(solution)/shard_map/cross_keys/pallas_call | solution.py:291
  775.2 194.4 %decode.2.refs_17_ = bf16[32,96,1024]{2,1,0:T(8,128)(2,1)} custom-call(s32[256]{0:T(256)} %copy-done.1, bf16[32,96,1024]{2,1,0:T(8,128)(2,1)} %refs_0_.3, bf16[4096,1024]{1,0:T(8,128)(2,1)} %get-tuple-element.13.refs_1_, bf16[4096,1024]{1,0:T(8,128)(2,1)} %get-tuple-element.14.refs_2_, bf16[4096,1024]{1,0:T(8,128)(2,1)} %get-tuple-element.15.refs_3_, ...), custom_call_target="tpu_custom_call" | custom-call | flops 89999998976 | bytes 100000000 | tf_op jit(solution)/shard_map/decode/pallas_call | solution.py:457
  969.6 207.8 %decode.3 = bf16[32,96,1024]{2,1,0:T(8,128)(2,1)} custom-call(s32[256]{0:T(256)} %copy-done.1, bf16[32,96,1024]{2,1,0:T(8,128)(2,1)} %refs_0_.3, bf16[4096,1024]{1,0:T(8,128)(2,1)} %get-tuple-element.13.refs_1_, bf16[4096,1024]{1,0:T(8,128)(2,1)} %get-tuple-element.14.refs_2_, ...), custom_call_target="tpu_custom_call", output_to_operand_aliasing={{}: (18, {})} | custom-call | flops 89999998976 | bytes 100000000 | tf_op jit(solution)/shard_map/decode/pallas_call | solution.py:457
Async XLA Ops:
  170.5 359.8 %collective-permute-start.1 = (bf16[2048,1024]{1,0:T(8,128)(2,1)}, bf16[2048,1024]{1,0:T(8,128)(2,1)}, u32[]{:S(2)}, u32[]{:S(2)}) collective-permute-start(bf16[2048,1024]{1,0:T(8,128)(2,1)} %encode.4), channel_id=1, source_target_pairs={{0,2},{1,3},{2,0},{3,1},{4,6},{5,7},{6,4},{7,5}} | collective-permute-start | bytes 12582920 | tf_op jit(solution)/shard_map/ppermute | solution.py:494
  352.9 177.4 %collective-permute-start.2 = (bf16[2048,1024]{1,0:T(8,128)(2,1)}, bf16[2048,1024]{1,0:T(8,128)(2,1)}, u32[]{:S(2)}, u32[]{:S(2)}) collective-permute-start(bf16[2048,1024]{1,0:T(8,128)(2,1)} %encode.5), channel_id=1, source_target_pairs={{0,2},{1,3},{2,0},{3,1},{4,6},{5,7},{6,4},{7,5}} | collective-permute-start | bytes 12582920 | tf_op jit(solution)/shard_map/ppermute | solution.py:494
  475.1 53.7 %copy-start = (s32[256]{0:T(256)S(1)}, s32[256]{0:T(256)}, u32[]{:S(2)}) copy-start(s32[256]{0:T(256)} %plan.1) | copy-start | bytes 3076
  475.2 137.8 %collective-permute-start.3 = (bf16[2048,1024]{1,0:T(8,128)(2,1)}, bf16[2048,1024]{1,0:T(8,128)(2,1)}, u32[]{:S(2)}, u32[]{:S(2)}) collective-permute-start(bf16[2048,1024]{1,0:T(8,128)(2,1)} %encode.6), channel_id=1, source_target_pairs={{0,2},{1,3},{2,0},{3,1},{4,6},{5,7},{6,4},{7,5}} | collective-permute-start | bytes 12582920 | tf_op jit(solution)/shard_map/ppermute | solution.py:494
  528.8 170.0 %collective-permute-start.4 = (bf16[2048,1024]{1,0:T(8,128)(2,1)}, bf16[2048,1024]{1,0:T(8,128)(2,1)}, u32[]{:S(2)}, u32[]{:S(2)}) collective-permute-start(bf16[2048,1024]{1,0:T(8,128)(2,1)} %encode.7), channel_id=1, source_target_pairs={{0,2},{1,3},{2,0},{3,1},{4,6},{5,7},{6,4},{7,5}} | collective-permute-start | bytes 12582920 | tf_op jit(solution)/shard_map/ppermute | solution.py:494
  528.8 177.6 %collective-permute-start = (s32[256]{0:T(256)S(1)}, s32[256]{0:T(256)S(1)}, u32[]{:S(2)}, u32[]{:S(2)}) collective-permute-start(s32[256]{0:T(256)S(1)} %copy-done), channel_id=1, source_target_pairs={{0,2},{1,3},{2,0},{3,1},{4,6},{5,7},{6,4},{7,5}} | collective-permute-start | bytes 3080 | tf_op jit(solution)/shard_map/ppermute | solution.py:489
  706.5 0.6 copy-start.1

commit v2 on v1

v2 whole, which is shorter than its diff:
```python
import functools

import jax
import jax.numpy as jnp
from jax import lax
from jax.experimental import pallas as pl
from jax.experimental.pallas import tpu as pltpu
from jax.sharding import PartitionSpec as P

BF16 = jnp.bfloat16
F32 = jnp.float32
I32 = jnp.int32

ROWS = 32
T_ENC = 256
T_DEC = 96
D = 1024
FF = 2816
PAIRS = 8
BIN = 512
NB = ROWS * T_ENC // BIN
CHUNKS = (4, 4, 2, 2, 4)
TN = 256
TF = 256
NS = 128
UNIT = 16
SCALE = 64 ** -0.5 * 1.4426950408889634
VMEM_MAX = 64 * 2**20 - 2**17

P_ORDER, P_OFF, P_LEN, P_GLOB, P_START, P_NBINS = 0, 32, 64, 96, 128, 160


def plan_kernel(len_ref, rank_ref, plan_ref, free, count, rbin, roff, rk, order):
    def clear(i, _):
        free[i] = BIN // UNIT
        count[i] = 0
        order[rank_ref[i]] = i
        order[rank_ref[i + NB]] = i + NB
        return 0

    lax.fori_loop(0, NB, clear, 0, unroll=4)

    def by_rank(i, _):
        r = order[i]
        size = (len_ref[r] + UNIT - 1) // UNIT
        b = lax.while_loop(lambda b: free[b] < size, lambda b: b + 1, jnp.int32(0))
        left = free[b]
        rbin[r] = b
        roff[r] = BIN - left * UNIT
        rk[r] = count[b]
        free[b] = left - size
        count[b] = count[b] + 1
        return 0

    lax.fori_loop(0, ROWS, by_rank, 0)

    def starts(b, carry):
        total, nbins = carry
        plan_ref[P_START + b] = total
        c = count[b]
        return total + c, nbins + jnp.where(c > 0, 1, 0)

    total, nbins = lax.fori_loop(0, NB, starts, (jnp.int32(0), jnp.int32(0)))
    plan_ref[P_START + NB] = total

    plan_ref[P_NBINS] = nbins

    def place(r, _):
        b = rbin[r]
        pos = plan_ref[P_START + b] + rk[r]
        plan_ref[P_ORDER + pos] = r
        plan_ref[P_OFF + pos] = roff[r]
        plan_ref[P_LEN + pos] = len_ref[r]
        plan_ref[P_GLOB + pos] = b * BIN + roff[r]
        return 0

    lax.fori_loop(0, ROWS, place, 0, unroll=4)


def make_plan(enc_len):
    units = (enc_len + UNIT - 1) // UNIT
    at = jnp.arange(ROWS)
    before = (units[None, :] > units[:, None]) | ((units[None, :] == units[:, None]) & (at[None, :] < at[:, None]))
    rank = jnp.sum(before.astype(I32), axis=1)
    smem = pl.BlockSpec(memory_space=pltpu.SMEM)
    return pl.pallas_call(
        plan_kernel,
        out_shape=jax.ShapeDtypeStruct((256,), I32),
        in_specs=[smem, smem],
        out_specs=smem,
        scratch_shapes=[pltpu.SMEM((32,), I32) for _ in range(6)],
        name="plan",
    )(enc_len, rank)


def norm_rows(src, dst, rows):
    step = NS
    for m in range(0, rows, step):
        v = src[m:m + step, :].astype(F32)
        inv = lax.rsqrt(jnp.mean(v * v, axis=-1, keepdims=True) + 1e-6)
        dst[m:m + step, :] = (v * inv).astype(BF16)


def gelu(x):
    inner = x * (x * x * (0.044715 * 0.7978845608028654) + 0.7978845608028654)
    half = x * 0.5
    return half + half * jnp.tanh(inner)


def attend_pair(q, k, v, mask, vmask=None):
    tq, tk = q.shape[0], k.shape[0]
    lane = lax.broadcasted_iota(I32, (tq, 128), 1)
    low = (lane < 64)
    lowf = low.astype(F32).astype(BF16)
    q2 = jnp.concatenate([q * lowf, q * (1 - lowf)], axis=0)
    s = lax.dot_general(q2, k, (((1,), (1,)), ((), ())), preferred_element_type=F32)
    s = jnp.where(mask, s, -1e30)
    top = jnp.max(s, axis=-1, keepdims=True)
    e = jnp.exp2((s - top) * SCALE).astype(BF16)
    if vmask is not None:
        v = jnp.where(vmask, v, jnp.zeros_like(v))
    va = jnp.concatenate([v, jnp.ones_like(v)], axis=1)
    o = jnp.dot(e, va, preferred_element_type=F32)
    num = jnp.where(low, o[:tq, :128], o[tq:, :128])
    den = jnp.where(low, o[:tq, 128:], o[tq:, 128:])
    return (num / den).astype(BF16)


def enc_kernel(base, plan, x_hbm, wq_h, wk_h, wv_h, wo_h, w1_h, w2_h, after, out_ref,
               xb, n_s, q_s, k_s, v_s, c_s, inner, wq, wk, wv, wo, w1, w2, xsem, wsem):
    i = pl.program_id(0)
    b = base + i
    nbins = plan[P_NBINS]
    slot = lax.rem(i, 2)
    weights = [(wq_h, wq), (wk_h, wk), (wv_h, wv), (wo_h, wo), (w1_h, w1), (w2_h, w2)]

    def weight_copy(j, l):
        return pltpu.make_async_copy(weights[j][0].at[l], weights[j][1].at[l], wsem.at[j, l])

    def row_copies(bb, sl, start):
        def per_row(pos, _):
            row, off = plan[P_ORDER + pos], plan[P_OFF + pos]
            units = (plan[P_LEN + pos] + UNIT - 1) // UNIT
            for bit in (16, 8, 4, 2, 1):
                @pl.when((units & bit) != 0)
                def _():
                    at = (units & ~(2 * bit - 1)) * UNIT
                    cp = pltpu.make_async_copy(
                        x_hbm.at[row, pl.ds(pl.multiple_of(at, UNIT), bit * UNIT), :],
                        xb.at[sl, pl.ds(pl.multiple_of(off + at, UNIT), bit * UNIT), :],
                        xsem.at[sl])
                    if start:
                        cp.start()
                    else:
                        cp.wait()
            return 0

        lax.fori_loop(plan[P_START + bb], plan[P_START + bb + 1], per_row, 0)

    @pl.when(jnp.logical_and(i == 0, b < nbins))
    def _():
        row_copies(b, slot, True)
        for l in range(2):
            for j in range(6):
                weight_copy(j, l).start()
        tail = slice(BIN, BIN + T_ENC)
        for ref in (q_s, k_s, v_s):
            ref[tail, :] = jnp.zeros((T_ENC, D), BF16)
        c_s[...] = jnp.zeros_like(c_s)

    @pl.when(jnp.logical_and(i + 1 < pl.num_programs(0), b + 1 < nbins))
    def _():
        row_copies(b + 1, 1 - slot, True)

    @pl.when(b >= nbins)
    def _():
        out_ref[...] = jnp.zeros_like(out_ref)

    @pl.when(b < nbins)
    def _():
        row_copies(b, slot, False)
        first, last = plan[P_START + b], plan[P_START + b + 1]
        used = plan[P_OFF + last - 1] + (plan[P_LEN + last - 1] + UNIT - 1) // UNIT * UNIT
        h = xb.at[slot]

        def zero_unit(u, _):
            h[pl.ds(pl.multiple_of(u * UNIT, UNIT), UNIT), :] = jnp.zeros((UNIT, D), BF16)
            return 0

        lax.fori_loop(used // UNIT, BIN // UNIT, zero_unit, 0)

        def need(j, l):
            @pl.when(i == 0)
            def _():
                weight_copy(j, l).wait()

        def layer(l, _):
            for j in range(3):
                need(j, l)
            norm_rows(h, n_s, BIN)
            for w, dst in ((wq, q_s), (wk, k_s), (wv, v_s)):
                for n in range(0, D, TN):
                    dst[0:BIN, n:n + TN] = jnp.dot(n_s[...], w[l, :, n:n + TN], preferred_element_type=F32).astype(BF16)

            def per_row(pos, _):
                off = pl.multiple_of(plan[P_OFF + pos], UNIT)
                length = plan[P_LEN + pos]

                def run(t):
                    mask = lax.broadcasted_iota(I32, (2 * t, T_ENC), 1) < length
                    for p in range(PAIRS):
                        cols = slice(p * 128, (p + 1) * 128)
                        c_s[pl.ds(off, t), cols] = attend_pair(
                            q_s[pl.ds(off, t), cols], k_s[pl.ds(off, T_ENC), cols], v_s[pl.ds(off, T_ENC), cols], mask)

                for t in range(96, T_ENC + 1, 32):
                    lo = 0 if t == 96 else t - 32

                    @pl.when(jnp.logical_and(length > lo, length <= t))
                    def _():
                        run(t)

                return 0

            lax.fori_loop(first, last, per_row, 0)
            for j in range(3, 6):
                need(j, l)
            for n in range(0, D, TN):
                u = jnp.dot(c_s[0:BIN, :], wo[l, :, n:n + TN], preferred_element_type=F32)
                h[:, n:n + TN] = (h[:, n:n + TN].astype(F32) + u).astype(BF16)
            norm_rows(h, n_s, BIN)
            for n in range(0, FF, TF):
                u = jnp.dot(n_s[...], w1[l, :, n:n + TF], preferred_element_type=F32)
                inner[:, n:n + TF] = gelu(u).astype(BF16)
            for n in range(0, D, TN):
                u = jnp.dot(inner[...], w2[l, :, n:n + TN], preferred_element_type=F32)
                h[:, n:n + TN] = (h[:, n:n + TN].astype(F32) + u).astype(BF16)
            return 0

        lax.fori_loop(0, 2, layer, 0)
        norm_rows(h, out_ref, BIN)


def encode_chunk(base, bins, plan, x_enc, weights, after):
    hbm = pl.BlockSpec(memory_space=pl.ANY)
    vm = lambda *s: pltpu.VMEM(s, BF16)
    tokens = BIN + T_ENC
    return pl.pallas_call(
        functools.partial(enc_kernel, base),
        out_shape=jax.ShapeDtypeStruct((bins * BIN, D), BF16),
        grid_spec=pltpu.PrefetchScalarGridSpec(
            num_scalar_prefetch=1,
            grid=(bins,),
            in_specs=[hbm] * 8,
            out_specs=pl.BlockSpec((BIN, D), lambda i, plan: (i, 0)),
            scratch_shapes=[
                vm(2, BIN, D), vm(BIN, D), vm(tokens, D), vm(tokens, D), vm(tokens, D), vm(tokens, D), vm(BIN, FF),
                vm(2, D, D), vm(2, D, D), vm(2, D, D), vm(2, D, D), vm(2, D, FF), vm(2, FF, D),
                pltpu.SemaphoreType.DMA((2,)), pltpu.SemaphoreType.DMA((6, 2)),
            ],
        ),
        compiler_params=pltpu.CompilerParams(vmem_limit_bytes=VMEM_MAX, dimension_semantics=("arbitrary",)),
        cost_estimate=pl.CostEstimate(flops=20_000_000_000 * bins, bytes_accessed=60_000_000, transcendentals=0),
        name="encode",
    )(plan, x_enc, *weights, after)


def cross_kernel(base, sizes, plan, *refs):
    h_hbm = refs[:len(sizes)]
    wk_ref, wv_ref, after, k_ref, v_ref, hb, hsem = refs[len(sizes):]
    i = pl.program_id(0)
    slot = lax.rem(i, 2)
    nbins = plan[P_NBINS] - base

    def fetch(at, sl, start):
        lo = 0
        for ref, size in zip(h_hbm, sizes):
            @pl.when(jnp.logical_and(at < nbins, jnp.logical_and(at >= lo, at < lo + size)))
            def _(ref=ref, lo=lo):
                cp = pltpu.make_async_copy(
                    ref.at[pl.ds(pl.multiple_of((at - lo) * BIN, BIN), BIN), :], hb.at[sl], hsem.at[sl])
                if start:
                    cp.start()
                else:
                    cp.wait()
            lo += size

    @pl.when(i == 0)
    def _():
        fetch(i, slot, True)

    @pl.when(i + 1 < sum(sizes))
    def _():
        fetch(i + 1, 1 - slot, True)

    fetch(i, slot, False)

    @pl.when(i < nbins)
    def _():
        for l in range(2):
            for w, dst in ((wk_ref, k_ref), (wv_ref, v_ref)):
                for n in range(0, D, TN):
                    dst[l, :, n:n + TN] = jnp.dot(hb[slot], w[l, :, n:n + TN], preferred_element_type=F32).astype(BF16)


def cross_keys(base, plan, hs, wk, wv, after):
    sizes = tuple(h.shape[0] // BIN for h in hs)
    tokens = sum(sizes) * BIN
    hbm = pl.BlockSpec(memory_space=pl.ANY)
    whole = pl.BlockSpec((2, D, D), lambda i, plan: (0, 0, 0))

    def block(i, plan):
        return 0, jnp.minimum(i, jnp.maximum(plan[P_NBINS] - 1 - base, 0)), 0

    spec = pl.BlockSpec((2, BIN, D), block)
    return pl.pallas_call(
        functools.partial(cross_kernel, base, sizes),
        out_shape=[jax.ShapeDtypeStruct((2, tokens + BIN, D), BF16)] * 2,
        grid_spec=pltpu.PrefetchScalarGridSpec(
            num_scalar_prefetch=1, grid=(sum(sizes),), in_specs=[hbm] * len(hs) + [whole, whole, hbm], out_specs=[spec] * 2,
            scratch_shapes=[pltpu.VMEM((2, BIN, D), BF16), pltpu.SemaphoreType.DMA((2,))]),
        compiler_params=pltpu.CompilerParams(vmem_limit_bytes=VMEM_MAX, dimension_semantics=("arbitrary",)),
        cost_estimate=pl.CostEstimate(flops=8 * tokens * D * D, bytes_accessed=10 * tokens * D, transcendentals=0),
        name="cross_keys",
    )(plan, *hs, wk, wv, after)


G = 8
MG = G * T_DEC
HALF = ROWS // 2
HALF_TOKENS = NB * BIN // 2


def dec_kernel(half, plan, *refs):
    nkv = half + 1
    y_hbm = refs[0]
    kv_hbm = refs[1:1 + 2 * nkv]
    w_hbm = refs[1 + 2 * nkv:9 + 2 * nkv]
    rest = refs[9 + 2 * nkv + (1 if half else 0):]
    out_hbm, zb, n_s, qkv, c_s, kb, vb = rest[:7]
    w_s = rest[7:15]
    ysem, osem, kvsem, wsem = rest[15:]
    inner = qkv.at[0:MG, 0:FF]
    wq, wk, wv, wo, cq, co, w1, w2 = w_s
    i = pl.program_id(0)
    groups = pl.num_programs(0)
    slot = lax.rem(i, 2)

    def weight_copy(j, l):
        return pltpu.make_async_copy(w_hbm[j].at[l], w_s[j].at[l], wsem.at[j, l])

    def first_row(g):
        return half * HALF + g * G

    def y_copy(g, sl, r):
        row = plan[P_ORDER + first_row(g) + r]
        return pltpu.make_async_copy(y_hbm.at[row], zb.at[sl, pl.ds(r * T_DEC, T_DEC), :], ysem.at[sl])

    def out_copy(g, sl, r):
        row = plan[P_ORDER + first_row(g) + r]
        return pltpu.make_async_copy(zb.at[sl, pl.ds(r * T_DEC, T_DEC), :], out_hbm.at[row], osem.at[sl])

    def kv_start(l, r):
        at = plan[P_GLOB + first_row(i) + r]
        sl = lax.rem(r, 2)
        for part in range(nkv):
            @pl.when(jnp.logical_and(at >= part * HALF_TOKENS, at < (part + 1) * HALF_TOKENS))
            def _():
                rows = pl.ds(pl.multiple_of(at - part * HALF_TOKENS, UNIT), T_ENC)
                pltpu.make_async_copy(kv_hbm[2 * part].at[l, rows, :], kb.at[sl], kvsem.at[0, sl]).start()
                pltpu.make_async_copy(kv_hbm[2 * part + 1].at[l, rows, :], vb.at[sl], kvsem.at[1, sl]).start()

    def kv_wait(l, r):
        sl = lax.rem(r, 2)
        pltpu.make_async_copy(kv_hbm[0].at[l, pl.ds(0, T_ENC), :], kb.at[sl], kvsem.at[0, sl]).wait()
        pltpu.make_async_copy(kv_hbm[1].at[l, pl.ds(0, T_ENC), :], vb.at[sl], kvsem.at[1, sl]).wait()

    @pl.when(i == 0)
    def _():
        qkv[MG:MG + 64, :] = jnp.zeros((64, 3 * D), BF16)
        for r in range(G):
            y_copy(0, 0, r).start()
        for l in range(2):
            for j in range(8):
                weight_copy(j, l).start()

    @pl.when(i >= 1)
    def _():
        for r in range(G):
            out_copy(i - 1, 1 - slot, r).wait()

    @pl.when(i + 1 < groups)
    def _():
        for r in range(G):
            y_copy(i + 1, 1 - slot, r).start()

    for r in range(G):
        y_copy(i, slot, r).wait()
    z = zb.at[slot]

    def need(j, l):
        @pl.when(i == 0)
        def _():
            weight_copy(j, l).wait()

    def add_to_z(src, w, l):
        for n in range(0, D, TN):
            u = jnp.dot(src[...], w[l, :, n:n + TN], preferred_element_type=F32)
            z[:, n:n + TN] = (z[:, n:n + TN].astype(F32) + u).astype(BF16)

    def layer(l, _):
        kv_start(l, jnp.int32(0))
        kv_start(l, jnp.int32(1))
        for j in range(3):
            need(j, l)
        norm_rows(z, n_s, MG)
        for j, w in enumerate((wq, wk, wv)):
            for n in range(0, D, TN):
                qkv[0:MG, j * D + n:j * D + n + TN] = jnp.dot(n_s[...], w[l, :, n:n + TN], preferred_element_type=F32).astype(BF16)
        two = 2 * T_DEC
        row_at = lax.broadcasted_iota(I32, (2 * two, T_ENC), 0)
        row_at = jnp.where(row_at >= two, row_at - two, row_at)
        col_at = lax.broadcasted_iota(I32, (2 * two, T_ENC), 1)
        causal = (row_at >= col_at) & ((row_at < T_DEC) | (col_at >= T_DEC))

        def self_rows(r, _):
            at = pl.multiple_of(r * two, 64)
            for p in range(PAIRS):
                cols = slice(p * 128, (p + 1) * 128)
                c_s[pl.ds(at, two), cols] = attend_pair(
                    qkv[pl.ds(at, two), p * 128:(p + 1) * 128],
                    qkv[pl.ds(at, T_ENC), D + p * 128:D + (p + 1) * 128],
                    qkv[pl.ds(at, T_ENC), 2 * D + p * 128:2 * D + (p + 1) * 128], causal)
            return 0

        lax.fori_loop(0, G // 2, self_rows, 0)
        need(3, l)
        need(4, l)
        add_to_z(c_s, wo, l)
        norm_rows(z, n_s, MG)
        for n in range(0, D, TN):
            qkv[0:MG, n:n + TN] = jnp.dot(n_s[...], cq[l, :, n:n + TN], preferred_element_type=F32).astype(BF16)

        def cross_row(r, _):
            kv_wait(l, r)
            sl = lax.rem(r, 2)
            length = plan[P_LEN + first_row(i) + r]
            mask = lax.broadcasted_iota(I32, (two, T_ENC), 1) < length
            vmask = lax.broadcasted_iota(I32, (T_ENC, 128), 0) < length
            rows = pl.ds(pl.multiple_of(r * T_DEC, 32), T_DEC)
            for p in range(PAIRS):
                cols = slice(p * 128, (p + 1) * 128)
                c_s[rows, cols] = attend_pair(qkv[rows, cols], kb[sl, :, cols], vb[sl, :, cols], mask, vmask)

            @pl.when(r + 2 < G)
            def _():
                kv_start(l, r + 2)

            return 0

        lax.fori_loop(0, G, cross_row, 0)
        for j in range(5, 8):
            need(j, l)
        add_to_z(c_s, co, l)
        norm_rows(z, n_s, MG)
        for n in range(0, FF, TF):
            u = jnp.dot(n_s[...], w1[l, :, n:n + TF], preferred_element_type=F32)
            inner[:, n:n + TF] = gelu(u).astype(BF16)
        add_to_z(inner, w2, l)
        return 0

    lax.fori_loop(0, 2, layer, 0)

    for r in range(G):
        out_copy(i, slot, r).start()

    @pl.when(i == groups - 1)
    def _():
        for r in range(G):
            out_copy(i, slot, r).wait()


def decode_half(half, plan, y_dec, kvs, weights, prev):
    hbm = pl.BlockSpec(memory_space=pl.ANY)
    vm = lambda *s: pltpu.VMEM(s, BF16)
    ins = [y_dec, *kvs, *weights] + ([prev] if half else [])
    return pl.pallas_call(
        functools.partial(dec_kernel, half),
        out_shape=jax.ShapeDtypeStruct((ROWS, T_DEC, D), BF16),
        grid_spec=pltpu.PrefetchScalarGridSpec(
            num_scalar_prefetch=1,
            grid=(HALF // G,),
            in_specs=[hbm] * len(ins),
            out_specs=hbm,
            scratch_shapes=[
                vm(2, MG, D), vm(MG, D), vm(MG + 64, 3 * D), vm(MG, D),
                vm(2, T_ENC, D), vm(2, T_ENC, D),
                vm(2, D, D), vm(2, D, D), vm(2, D, D), vm(2, D, D), vm(2, D, D), vm(2, D, D), vm(2, D, FF), vm(2, FF, D),
                pltpu.SemaphoreType.DMA((2,)), pltpu.SemaphoreType.DMA((2,)), pltpu.SemaphoreType.DMA((2, 2)),
                pltpu.SemaphoreType.DMA((8, 2)),
            ],
        ),
        input_output_aliases={len(ins): 0} if half else {},
        compiler_params=pltpu.CompilerParams(vmem_limit_bytes=VMEM_MAX, dimension_semantics=("arbitrary",)),
        cost_estimate=pl.CostEstimate(flops=90_000_000_000, bytes_accessed=100_000_000, transcendentals=0),
        name="decode",
    )(plan, *ins)


def solution(mesh):
    pair_size = mesh.shape["pair"]
    to_partner = [(source, (source + pair_size // 2) % pair_size) for source in range(pair_size)]
    row_spec = P(("data", "pair"))
    full_spec = P()

    def per_device(x_enc, enc_len, y_dec, enc_wq, enc_wk, enc_wv, enc_wo, enc_w1, enc_w2, dec_wq, dec_wk, dec_wv, dec_wo, crs_wq, crs_wk, crs_wv, crs_wo, dec_w1, dec_w2):
        flat = lambda w: w.reshape(2, D, D)
        plan = make_plan(enc_len)
        partner_plan = lax.ppermute(plan, "pair", to_partner)
        enc_weights = (enc_wq, enc_wk, enc_wv, flat(enc_wo), enc_w1, enc_w2)
        enc_out, base, h = [], 0, x_enc
        for bins in CHUNKS:
            h = encode_chunk(base, bins, plan, x_enc, enc_weights, h)
            enc_out.append(lax.ppermute(h, "pair", to_partner))
            base += bins
        dec_weights = (dec_wq, dec_wk, dec_wv, flat(dec_wo), crs_wq, flat(crs_wo), dec_w1, dec_w2)
        out, kvs, after = None, [], h
        for half in range(2):
            hs = enc_out[2:] if half else enc_out[:2]
            kvs += cross_keys(half * NB // 2, partner_plan, hs, crs_wk, crs_wv, after)
            out = decode_half(half, partner_plan, y_dec, kvs, dec_weights, out)
            after = out
        return out

    return jax.shard_map(per_device, mesh=mesh, in_specs=(row_spec, row_spec, row_spec) + (full_spec,) * 16, out_specs=row_spec, check_vma=False)
```

time: 1180 us -> 790 us (0.67)
  the two profiles are of different devices: /device:TPU:7 before, /device:TPU:4 now
where the time goes in v2:
time: 790 us; the launch traced here: 777 us
  Pallas kernels  738 us (93%)
  starting transfers between devices  37.5 us (5%)
    pallas_call x5, Pallas kernels, encode_chunk(): pl.pallas_call(functools.partial(enc_kernel, base), out_shape=jax.ShapeDt...  360 us
    pallas_call x2, Pallas kernels, decode_half(): pl.pallas_call(functools.partial(dec_kernel, half), out_shape=jax.ShapeDt...  303 us
    pallas_call x2, Pallas kernels, cross_keys(): pl.pallas_call(functools.partial(cross_kernel, base, sizes), out_shape=[j...  70.2 us
    ppermute x5, starting transfers between devices, per_device(): enc_out.append(lax.ppermute(h, 'pair', to_partner))  35.8 us
  transfers between devices with their start and end apart: 6, of which 0 were waited for; matrix products, arithmetic and copies ran while one was open for 0% of the time, Pallas kernels for 72%

profile of v2, /device:TPU:4, one launch (start us, length us, event | category | flops | bytes accessed | tf_op | source)
XLA Modules:
  0.0 777.0 jit_solution(4052935016142820806)
XLA Ops:
  0.0 0.7 and_select_fusion
  0.7 0.7 convert_reduce_fusion.rank_ref
  1.4 3.9 plan.1
  5.3 1.7 collective-permute-start
  7.0 124.9 %encode.5.after = bf16[2048,1024]{1,0:T(8,128)(2,1)} custom-call(s32[256]{0:T(256)} %plan.1, bf16[32,256,1024]{2,1,0:T(8,128)(2,1)} %x_hbm.9, bf16[2,1024,1024]{2,1,0:T(8,128)(2,1)} %wq_h.9, bf16[2,1024,1024]{2,1,0:T(8,128)(2,1)} %wk_h.9, bf16[2,1024,1024]{2,1,0:T(8,128)(2,1)} %wv_h.9, bf16[2,1024,1024]{2,1,0:T(8,128)(2,1)} %bitcast.3, ...), custom_call_target="tpu_custom_call" | custom-call | flops 80000000000 | bytes 60000000 | tf_op jit(solution)/shard_map/encode/pallas_call | solution.py:248
  132.0 0.0 collective-permute-start.1
  132.0 128.0 %encode.6.after = bf16[2048,1024]{1,0:T(8,128)(2,1)} custom-call(s32[256]{0:T(256)} %plan.1, bf16[32,256,1024]{2,1,0:T(8,128)(2,1)} %x_hbm.9, bf16[2,1024,1024]{2,1,0:T(8,128)(2,1)} %wq_h.9, bf16[2,1024,1024]{2,1,0:T(8,128)(2,1)} %wk_h.9, bf16[2,1024,1024]{2,1,0:T(8,128)(2,1)} %wv_h.9, bf16[2,1024,1024]{2,1,0:T(8,128)(2,1)} %bitcast.4, ...), custom_call_target="tpu_custom_call" | custom-call | flops 80000000000 | bytes 60000000 | tf_op jit(solution)/shard_map/encode/pallas_call | solution.py:248
  260.0 0.0 collective-permute-start.2
  260.1 68.7 %encode.7.after = bf16[1024,1024]{1,0:T(8,128)(2,1)} custom-call(s32[256]{0:T(256)} %plan.1, bf16[32,256,1024]{2,1,0:T(8,128)(2,1)} %x_hbm.9, bf16[2,1024,1024]{2,1,0:T(8,128)(2,1)} %wq_h.9, bf16[2,1024,1024]{2,1,0:T(8,128)(2,1)} %wk_h.9, bf16[2,1024,1024]{2,1,0:T(8,128)(2,1)} %wv_h.9, bf16[2,1024,1024]{2,1,0:T(8,128)(2,1)} %bitcast.5, ...), custom_call_target="tpu_custom_call" | custom-call | flops 40000000000 | bytes 60000000 | tf_op jit(solution)/shard_map/encode/pallas_call | solution.py:248
  328.8 0.1 collective-permute-start.3
  328.9 34.6 %encode.8.after = bf16[1024,1024]{1,0:T(8,128)(2,1)} custom-call(s32[256]{0:T(256)} %plan.1, bf16[32,256,1024]{2,1,0:T(8,128)(2,1)} %x_hbm.9, bf16[2,1024,1024]{2,1,0:T(8,128)(2,1)} %wq_h.9, bf16[2,1024,1024]{2,1,0:T(8,128)(2,1)} %wk_h.9, bf16[2,1024,1024]{2,1,0:T(8,128)(2,1)} %wv_h.9, bf16[2,1024,1024]{2,1,0:T(8,128)(2,1)} %bitcast.6, ...), custom_call_target="tpu_custom_call" | custom-call | flops 40000000000 | bytes 60000000 | tf_op jit(solution)/shard_map/encode/pallas_call | solution.py:248
  363.5 35.6 %collective-permute-start.4 = (bf16[1024,1024]{1,0:T(8,128)(2,1)}, bf16[1024,1024]{1,0:T(8,128)(2,1)}, u32[]{:S(2)}, u32[]{:S(2)}) collective-permute-start(bf16[1024,1024]{1,0:T(8,128)(2,1)} %encode.8.after), channel_id=1, source_target_pairs={{0,2},{1,3},{2,0},{3,1},{4,6},{5,7},{6,4},{7,5}} | collective-permute-start | bytes 6291464 | tf_op jit(solution)/shard_map/ppermute | solution.py:524
  399.0 4.1 encode.9.refs_4_
  403.1 0.0 collective-permute-done.plan
  403.1 0.0 collective-permute-start.5
  403.2 0.0 collective-permute-done.2.refs_1_
  403.2 0.0 collective-permute-done.1.refs_0_
  403.2 44.1 %cross_keys.2 = (bf16[2,4608,1024]{2,1,0:T(8,128)(2,1)}, bf16[2,4608,1024]{2,1,0:T(8,128)(2,1)}) custom-call(s32[256]{0:T(256)} %collective-permute-done.plan, bf16[2048,1024]{1,0:T(8,128)(2,1)} %collective-permute-done.1.refs_0_, bf16[2048,1024]{1,0:T(8,128)(2,1)} %collective-permute-done.2.refs_1_, bf16[2,1024,1024]{2,1,0:T(8,128)(2,1)} %refs_3_.5, ...), custom_call_target="tpu_custom_call" | custom-call | flops 34359738368 | bytes 41943040 | tf_op jit(solution)/shard_map/cross_keys/pallas_call | solution.py:316
  447.3 151.9 %decode.2.refs_5_.refs_13_ = bf16[32,96,1024]{2,1,0:T(8,128)(2,1)} custom-call(s32[256]{0:T(256)} %collective-permute-done.plan, bf16[32,96,1024]{2,1,0:T(8,128)(2,1)} %refs_0_.3, bf16[2,4608,1024]{2,1,0:T(8,128)(2,1)} %get-tuple-element.9.refs_1_, bf16[2,4608,1024]{2,1,0:T(8,128)(2,1)} %get-tuple-element.10.refs_2_, bf16[2,1024,1024]{2,1,0:T(8,128)(2,1)} %refs_5_.3, ...), custom_call_target="tpu_custom_call" | custom-call | flops 89999998976 | bytes 100000000 | tf_op jit(solution)/shard_map/decode/pallas_call | solution.py:487
  599.2 0.0 collective-permute-done.4.refs_1_
  599.2 0.0 collective-permute-done.3.refs_0_
  599.2 0.0 collective-permute-done.5.refs_2_
  599.2 26.1 %cross_keys.3 = (bf16[2,4608,1024]{2,1,0:T(8,128)(2,1)}, bf16[2,4608,1024]{2,1,0:T(8,128)(2,1)}) custom-call(s32[256]{0:T(256)} %collective-permute-done.plan, bf16[1024,1024]{1,0:T(8,128)(2,1)} %collective-permute-done.3.refs_0_, bf16[1024,1024]{1,0:T(8,128)(2,1)} %collective-permute-done.4.refs_1_, bf16[2048,1024]{1,0:T(8,128)(2,1)} %collective-permute-done.5.refs_2_, ...), custom_call_target="tpu_custom_call" | custom-call | flops 34359738368 | bytes 41943040 | tf_op jit(solution)/shard_map/cross_keys/pallas_call | solution.py:316
  625.3 151.5 %decode.3 = bf16[32,96,1024]{2,1,0:T(8,128)(2,1)} custom-call(s32[256]{0:T(256)} %collective-permute-done.plan, bf16[32,96,1024]{2,1,0:T(8,128)(2,1)} %refs_0_.3, bf16[2,4608,1024]{2,1,0:T(8,128)(2,1)} %get-tuple-element.9.refs_1_, bf16[2,4608,1024]{2,1,0:T(8,128)(2,1)} %get-tuple-element.10.refs_2_, ...), custom_call_target="tpu_custom_call", output_to_operand_aliasing={{}: (14, {})} | custom-call | flops 89999998976 | bytes 100000000 | tf_op jit(solution)/shard_map/decode/pallas_call | solution.py:487
Async XLA Ops:
  5.3 397.9 %collective-permute-start = (s32[256]{0:T(256)}, s32[256]{0:T(256)}, u32[]{:S(2)}, u32[]{:S(2)}) collective-permute-start(s32[256]{0:T(256)} %plan.1), channel_id=1, source_target_pairs={{0,2},{1,3},{2,0},{3,1},{4,6},{5,7},{6,4},{7,5}} | collective-permute-start | bytes 3080 | tf_op jit(solution)/shard_map/ppermute | solution.py:519
  132.0 271.2 %collective-permute-start.1 = (bf16[2048,1024]{1,0:T(8,128)(2,1)}, bf16[2048,1024]{1,0:T(8,128)(2,1)}, u32[]{:S(2)}, u32[]{:S(2)}) collective-permute-start(bf16[2048,1024]{1,0:T(8,128)(2,1)} %encode.5.after), channel_id=1, source_target_pairs={{0,2},{1,3},{2,0},{3,1},{4,6},{5,7},{6,4},{7,5}} | collective-permute-start | bytes 12582920 | tf_op jit(solution)/shard_map/ppermute | solution.py:524
  260.0 143.2 %collective-permute-start.2 = (bf16[2048,1024]{1,0:T(8,128)(2,1)}, bf16[2048,1024]{1,0:T(8,128)(2,1)}, u32[]{:S(2)}, u32[]{:S(2)}) collective-permute-start(bf16[2048,1024]{1,0:T(8,128)(2,1)} %encode.6.after), channel_id=1, source_target_pairs={{0,2},{1,3},{2,0},{3,1},{4,6},{5,7},{6,4},{7,5}} | collective-permute-start | bytes 12582920 | tf_op jit(solution)/shard_map/ppermute | solution.py:524
  328.8 270.5 %collective-permute-start.3 = (bf16[1024,1024]{1,0:T(8,128)(2,1)}, bf16[1024,1024]{1,0:T(8,128)(2,1)}, u32[]{:S(2)}, u32[]{:S(2)}) collective-permute-start(bf16[1024,1024]{1,0:T(8,128)(2,1)} %encode.7.after), channel_id=1, source_target_pairs={{0,2},{1,3},{2,0},{3,1},{4,6},{5,7},{6,4},{7,5}} | collective-permute-start | bytes 6291464 | tf_op jit(solution)/shard_map/ppermute | solution.py:524
  363.5 235.7 %collective-permute-start.4 = (bf16[1024,1024]{1,0:T(8,128)(2,1)}, bf16[1024,1024]{1,0:T(8,128)(2,1)}, u32[]{:S(2)}, u32[]{:S(2)}) collective-permute-start(bf16[1024,1024]{1,0:T(8,128)(2,1)} %encode.8.after), channel_id=1, source_target_pairs={{0,2},{1,3},{2,0},{3,1},{4,6},{5,7},{6,4},{7,5}} | collective-permute-start | bytes 6291464 | tf_op jit(solution)/shard_map/ppermute | solution.py:524
  403.1 196.1 %collective-permute-start.5 = (bf16[2048,1024]{1,0:T(8,128)(2,1)}, bf16[2048,1024]{1,0:T(8,128)(2,1)}, u32[]{:S(2)}, u32[]{:S(2)}) collective-permute-start(bf16[2048,1024]{1,0:T(8,128)(2,1)} %encode.9.refs_4_), channel_id=1, source_target_pairs={{0,2},{1,3},{2,0},{3,1},{4,6},{5,7},{6,4},{7,5}} | collective-permute-start | bytes 12582920 | tf_op jit(solution)/shard_map/ppermute | solution.py:524
